TPU v7x, 32 devices: a whole 2x2x4 slice. The times are simulated.
32 devices in a mesh: mem: 4 (over y, x), tile: 8 (over z, core).
Axes of the slice: x: 2, y: 2, z: 4, core: 2. Of those that a mesh axis runs over, the one named last changes fastest.
Arguments:
- ensemble: float32 [1024, 3, 64, 256], P('mem', None, 'tile'), may hold values from -4.5 to 5
- obs_cells: int32 [8, 256], replicated, may hold values from 0 to 6143
- region_tile: int32 [8], replicated, may hold values from 0 to 7, each once
- obs_values: float32 [8, 256], replicated, may hold values from -5.6 to 5.6
- obs_error: float32 [8, 256], replicated, may hold values from 0.05 to 0.75
Outputs:
- analysis: float32 [1024, 3, 64, 256], P('mem', None, 'tile')
Inputs may be any that keep to these rules, and one draw needn't show every extreme that they name: `obs_cells`: row r lists flat indices into the values of tile region_tile[r], ordered by field, then row within the tile, then column; indices may repeat. `region_tile`: each tile holds exactly one region.
All inputs are finite; a program needn't handle non-finite values.
Results may differ from a plain program's by a relative error of at most 0.00029.
Values sent between devices are 32-bit elements; how exact they have to be, the bound alone decides.
No kernel may reach another device: no remote copies, remote signals or barrier semaphores. Data moves between devices by JAX's collectives and lax.ppermute only.
A program may use at most 128 MiB of HBM per device.

v0:
```python
import functools
import math

import jax
import jax.numpy as jnp
from jax import lax
from jax.experimental import pallas as pl
from jax.experimental.pallas import tpu as pltpu
from jax.sharding import PartitionSpec as P


STEPS = 4
DEGREE = 4
FIELDS = 3
LANES = 128
CHUNKS = 4
VMEM_MIB = 22
SPREAD_VMEM_MIB = 58
REST_VMEM_MIB = 22
FIRST = 2
SPARE = 8
HIGHEST = lax.Precision.HIGHEST


F32 = jnp.float32
BF16 = jnp.bfloat16


def params(mib=VMEM_MIB):
    return pltpu.CompilerParams(vmem_limit_bytes=mib * 1024 * 1024)


def split2(x):
    high = x.astype(BF16)
    return high, (x - high.astype(F32)).astype(BF16)


def dot(a, b):
    return lax.dot_general(a, b, (((1,), (0,)), ((), ())), preferred_element_type=F32)


def dot_full(a, b):
    return lax.dot_general(
        a, b, (((1,), (0,)), ((), ())), precision=HIGHEST, preferred_element_type=F32
    )


def spread_body(x_ref, *refs, chunks, rows):
    outs, (staged, sems) = refs[: 2 * len(chunks)], refs[2 * len(chunks) :]
    stride = FIELDS * rows
    halves = staged.shape[0]
    copies, at = [], 0
    for index, (begin, size) in enumerate(chunks):
        for k in range(halves):
            copies.append(
                pltpu.make_async_copy(
                    x_ref.at[pl.ds(begin * stride, size * stride), pl.ds(k * LANES, LANES)],
                    staged.at[k, pl.ds(at * stride, size * stride)],
                    sems.at[index * halves + k],
                )
            )
        at += size
    for copy in copies:
        copy.start()
    at = 0
    for index, (begin, size) in enumerate(chunks):
        for k in range(halves):
            copies[index * halves + k].wait()
            for field in range(FIELDS):
                for row in range(rows):
                    out = outs[2 * index + row // (rows // 2)]
                    first = at * stride + field * rows + row
                    value = staged[k, pl.ds(first, size, stride=stride), :]
                    value = value + 1.0 if field == 0 else value * 1.5
                    slot = field * (rows // 2) + row % (rows // 2)
                    out[slot, :, k * LANES : (k + 1) * LANES] = value
        at += size


def spread(flat, chunks, rows, width, mib):
    half = FIELDS * (rows // 2)
    halves = width // LANES
    total = sum(size for _, size in chunks)
    shapes = [jax.ShapeDtypeStruct((half, size, width), F32) for _, size in chunks for _ in (0, 1)]
    out = pl.pallas_call(
        functools.partial(spread_body, chunks=chunks, rows=rows),
        in_specs=[pl.BlockSpec(memory_space=pl.ANY)],
        out_specs=[pl.BlockSpec(memory_space=pltpu.VMEM)] * len(shapes),
        out_shape=shapes,
        scratch_shapes=[
            pltpu.VMEM((halves, total * FIELDS * rows, LANES), F32),
            pltpu.SemaphoreType.DMA((halves * len(chunks),)),
        ],
        compiler_params=params(mib),
        name="spread",
    )(flat)
    return [(out[2 * i], out[2 * i + 1]) for i in range(len(chunks))]


def shifted(x, width):
    return pltpu.roll(x, width - 1, 1), pltpu.roll(x, 1, 1)


def prepared(h, u, v):
    vm, vp = 1.0 - v, 1.0 + v
    return h, u, v, vm, vp, h * vm, h * vp


def advance_row(south, middle, north, width, last):
    hs, us, vs, _, _, _, flow_s = south
    h, u, v, vm, vp, _, _ = middle
    hn, un, vn, _, _, flow_n, _ = north
    he, hw = shifted(h, width)
    ue, uw = shifted(u, width)
    ve, vw = shifted(v, width)
    um, up = 1.0 - u, 1.0 + u
    h_sum = (he * (1.0 - ue) + hw * (1.0 + uw)) + (flow_n + flow_s)
    u_sum = (ue * um + uw * up) + (un * vm + us * vp)
    v_sum = (ve * um + vw * up) + (vn * vm + vs * vp)
    h_new = 0.6 * h + 0.1 * h_sum
    u_new = (0.6 * u + 0.15 * v) + 0.1 * u_sum - 0.225 * (he - hw)
    v_new = (0.6 * v - 0.15 * u) + 0.1 * v_sum - 0.225 * (hn - hs)
    if last:
        return h_new - 1.0, u_new * (2.0 / 3.0), v_new * (2.0 / 3.0)
    return h_new, u_new, v_new


def owned_runs(units, parts, rows):
    each = units // parts
    whole = each // rows * rows
    runs = [(whole, 0), (each - whole, parts * whole)]
    return [run for run in runs if run[0]]


def forecast_body(
    me_ref, prev_ref, top_ref, bot_ref, next_ref, onehot_ref, *refs, begin, rows, size, block,
    width, parts, obs
):
    work, kept, onehot, sem, state_sems = refs[-5:]
    state_ref, *sends = refs[-6 - parts : -5]
    half = rows // 2
    total = rows + 2 * STEPS
    sources = (prev_ref, top_ref, bot_ref, next_ref)
    halves = width // LANES
    units = FIELDS * rows * halves
    each = units // parts
    place = pl.program_id(0)
    fetch = pltpu.make_async_copy(onehot_ref, onehot, sem)

    @pl.when(place == 0)
    def _():
        fetch.start()

    def group(index, carry):
        members = pl.ds(pl.multiple_of(index * 8, 8), 8)
        kept_members = pl.ds(pl.multiple_of(place * block + index * 8, 8), 8)

        def first(row):
            ref = sources[row // half]
            return prepared(*(ref[f * half + row % half, members, :] for f in range(FIELDS)))

        def later(step):
            return lambda row: prepared(
                *(work[(step - 1) % 2, f * total + row] for f in range(FIELDS))
            )

        for step in range(STEPS):
            load = first if step == 0 else later(step)
            last = step == STEPS - 1
            lo, hi = step + 1, total - 1 - step
            window = [load(lo - 1), load(lo)]
            for row in range(lo, hi):
                window.append(load(row + 1))
                new = advance_row(window[0], window[1], window[2], width, last)
                window.pop(0)
                for f in range(FIELDS):
                    if last:
                        for k in range(halves):
                            unit = (f * halves + k) * rows + row - STEPS
                            value = new[f][:, k * LANES : (k + 1) * LANES]
                            kept[unit, kept_members, :] = value
                    else:
                        work[step % 2, f * total + row] = new[f]
        return carry

    lax.fori_loop(0, block // 8, group, 0)

    def keep(index):
        source = pl.ds(pl.multiple_of(index * block, 8), block)
        target = pl.ds(pl.multiple_of(begin + index * block, 8), block)
        return pltpu.make_async_copy(
            kept.at[:, source, :], state_ref.at[:, target, :], state_sems.at[index]
        )

    keep(place).start()

    @pl.when(place == pl.num_programs(0) - 1)
    def _():
        fetch.wait()
        observed = jnp.zeros((size, obs), F32)
        for f in range(FIELDS):
            for row in range(rows):
                x = jnp.concatenate(
                    [kept[(f * halves + k) * rows + row] for k in range(halves)], axis=1
                )
                high = x.astype(BF16)
                rest = x - high.astype(F32)
                mid = rest.astype(BF16)
                low = (rest - mid.astype(F32)).astype(BF16)
                stacked = jnp.concatenate([high, mid, low], axis=0)
                part = dot(stacked, onehot[f * rows + row])
                observed = observed + ((part[:size] + part[size : 2 * size]) + part[2 * size :])
        me = me_ref[0]
        for p in range(parts):
            slot = 0
            for count, base in owned_runs(units, parts, rows):
                for j in range(count):
                    sends[p][slot] = kept[base + (me ^ p) * count + j]
                    slot += 1
            for k in range(obs // LANES):
                sends[p][each + k] = observed[:, k * LANES : (k + 1) * LANES]
        for index in range(size // block):
            keep(index).wait()


def forecast_chunk(
    me, prev, top, bot, nxt, onehot, state, begin, size, members, rows, width, parts, obs
):
    units = FIELDS * rows * (width // LANES)
    each = units // parts + obs // LANES
    half = FIELDS * (rows // 2)
    block = 16 if size % 16 == 0 else 8
    extra = [] if state is None else [state]
    return pl.pallas_call(
        functools.partial(
            forecast_body, begin=begin, rows=rows, size=size, block=block, width=width,
            parts=parts, obs=obs
        ),
        grid=(size // block,),
        in_specs=[pl.BlockSpec(memory_space=pltpu.SMEM)]
        + [pl.BlockSpec((half, block, width), lambda i: (0, i, 0))] * 4
        + [pl.BlockSpec(memory_space=pl.ANY)] * (1 + len(extra)),
        out_specs=[pl.BlockSpec(memory_space=pl.ANY)]
        + [pl.BlockSpec((each, size, LANES), lambda i: (0, 0, 0))] * parts,
        out_shape=[jax.ShapeDtypeStruct((units, SPARE * members, LANES), F32)]
        + [jax.ShapeDtypeStruct((each, size, LANES), F32)] * parts,
        scratch_shapes=[
            pltpu.VMEM((2, FIELDS * (rows + 2 * STEPS), 8, width), F32),
            pltpu.VMEM((units, size, LANES), F32),
            pltpu.VMEM(onehot.shape, BF16),
            pltpu.SemaphoreType.DMA,
            pltpu.SemaphoreType.DMA((size // block,)),
        ],
        compiler_params=params(),
        cost_estimate=pl.CostEstimate(flops=50_000_000, bytes_accessed=8_000_000, transcendentals=0),
        input_output_aliases={6: 0} if extra else {},
        name="forecast",
    )(me, prev, top, bot, nxt, onehot, *extra)


def joined_observed(blocks, each, obs):
    return jnp.concatenate(
        [
            jnp.concatenate([ref[each + k] for k in range(obs // LANES)], axis=1)
            for ref in blocks
        ],
        axis=0,
    )


def centred_products(blocks, each, obs, emit):
    scale = 1.0 / sum(ref.shape[1] for ref in blocks)
    y = joined_observed(blocks, each, obs)
    y_mean = jnp.sum(y, axis=0, keepdims=True) * scale
    perturbed = y - y_mean
    squares = jnp.sum(perturbed * perturbed, axis=0, keepdims=True)
    high, low = split2(perturbed.T)
    both = jnp.concatenate([high, low], axis=0)
    count = each + obs // LANES
    step = 2 if count % 2 == 0 else 1
    for unit in range(0, count, step):
        x = jnp.concatenate(
            [jnp.concatenate([ref[unit + k] for ref in blocks], axis=0) for k in range(step)],
            axis=1,
        )
        x_mean = jnp.sum(x, axis=0, keepdims=True) * scale
        d_high, d_low = split2(x - x_mean)
        part = dot(both, d_high)
        product = (part[:obs] + part[obs:]) + dot(high, d_low)
        for k in range(step):
            lanes = slice(k * LANES, (k + 1) * LANES)
            emit(unit + k, product[:, lanes], x_mean[:, lanes])
    return y_mean, squares


def early_body(*refs, count, each, obs):
    blocks = refs[:count]
    product_ref, mean_ref, y_ref = refs[count:]

    def emit(unit, product, mean):
        product_ref[unit] = product
        mean_ref[unit : unit + 1, :] = mean

    y_mean, squares = centred_products(blocks, each, obs, emit)
    y_ref[0:1, :] = y_mean
    y_ref[1:2, :] = squares


def early_covariance(blocks, each, obs):
    vmem = pl.BlockSpec(memory_space=pltpu.VMEM)
    return pl.pallas_call(
        functools.partial(early_body, count=len(blocks), each=each, obs=obs),
        in_specs=[vmem] * len(blocks),
        out_specs=[vmem] * 3,
        out_shape=[
            jax.ShapeDtypeStruct((each + obs // LANES, obs, LANES), F32),
            jax.ShapeDtypeStruct((each + obs // LANES, LANES), F32),
            jax.ShapeDtypeStruct((2, obs), F32),
        ],
        compiler_params=params(),
        cost_estimate=pl.CostEstimate(
            flops=10_000_000, bytes_accessed=8_000_000, transcendentals=0
        ),
        name="early",
    )(*blocks)


def late_body(
    target_ref, variance_ref, product_ref, mean_ref, y_ref, *refs, count, each, obs, first, before
):
    blocks = refs[:count]
    first_ref, second_ref, sums_ref, y_mean_ref, gram_ref = refs[count:]
    after = sum(ref.shape[1] for ref in blocks)
    total = before + after
    share = after / total
    cross = before * share
    y_late = jnp.sum(joined_observed(blocks, each, obs), axis=0, keepdims=True) * (1.0 / after)
    y_shift = y_late - y_ref[0:1, :]
    column = jnp.broadcast_to(cross * y_shift, (8, obs)).T[:, 0:1]

    def emit(unit, product, mean):
        old = mean_ref[unit : unit + 1, :]
        shift = mean - old
        value = product_ref[unit] + product + column * shift
        if unit >= each:
            gram_ref[:, (unit - each) * LANES : (unit - each + 1) * LANES] = value
            return
        out, at = (first_ref, unit) if unit < first else (second_ref, unit - first)
        out[at * obs : (at + 1) * obs, :] = value
        tail = (first if unit < first else each - first) * obs + at
        out[tail : tail + 1, :] = old + share * shift

    _, squares = centred_products(blocks, each, obs, emit)
    y_mean = y_ref[0:1, :] + share * y_shift
    misfit = target_ref[...] - y_mean
    spread = (y_ref[1:2, :] + squares + cross * y_shift * y_shift) / (total - 1)
    sums_ref[0:1, :] = misfit * misfit
    sums_ref[1:2, :] = spread + variance_ref[...]
    y_mean_ref[...] = jnp.broadcast_to(y_mean, y_mean_ref.shape)


def padded(count):
    return -(-count // 8) * 8


def late_covariance(target, variance, early, blocks, each, obs, before):
    vmem = pl.BlockSpec(memory_space=pltpu.VMEM)
    first = (each + 1) // 2
    second = each - first
    return pl.pallas_call(
        functools.partial(
            late_body, count=len(blocks), each=each, obs=obs, first=first, before=before
        ),
        in_specs=[vmem] * (5 + len(blocks)),
        out_specs=[vmem] * 5,
        out_shape=[
            jax.ShapeDtypeStruct((first * obs + padded(first), LANES), F32),
            jax.ShapeDtypeStruct((second * obs + padded(second), LANES), F32),
            jax.ShapeDtypeStruct((2, obs), F32),
            jax.ShapeDtypeStruct((8, obs), F32),
            jax.ShapeDtypeStruct((obs, obs), F32),
        ],
        compiler_params=params(),
        cost_estimate=pl.CostEstimate(
            flops=10_000_000, bytes_accessed=8_000_000, transcendentals=0
        ),
        name="late",
    )(target, variance, *early, *blocks)


def weights_body(
    sums_ref, target_ref, variance_ref, mean_ref, gram_ref, *refs, count, obs, total
):
    tails = obs // LANES
    blocks = [refs[i * tails : (i + 1) * tails] for i in range(count)]
    weights_ref, scale_ref = refs[count * tails :]

    def observed(slabs):
        return jnp.concatenate([slab[0] for slab in slabs], axis=1)

    y_mean = mean_ref[0:1, :]
    inflation = sums_ref[0:1, 0:1] / sums_ref[0:1, 1:2]
    factor = inflation / (total - 1)
    variance = variance_ref[...]
    weighted = (target_ref[...] - y_mean) / variance
    gram = gram_ref[...]
    g_row = jnp.sqrt(factor / variance)
    eye = (
        lax.broadcasted_iota(jnp.int32, (obs, obs), 0)
        == lax.broadcasted_iota(jnp.int32, (obs, obs), 1)
    ).astype(F32)
    g_col = jnp.sum(eye * g_row, axis=1, keepdims=True)
    kernel = gram * g_row * g_col
    norm = jnp.sum(jnp.sum(kernel * kernel, axis=1, keepdims=True), axis=0, keepdims=True)
    bound = 2.0 + jnp.sqrt(norm)
    slope = 2.0 / (bound - 1.0)
    angles = [(j + 0.5) * (math.pi / (DEGREE + 1)) for j in range(DEGREE + 1)]
    values = [
        lax.rsqrt(0.5 * (bound + 1.0) + 0.5 * (bound - 1.0) * math.cos(angle))
        for angle in angles
    ]
    coeffs = []
    for k in range(DEGREE + 1):
        term = sum(math.cos(k * angle) * value for angle, value in zip(angles, values))
        coeffs.append((2.0 if k else 1.0) / (DEGREE + 1) * term)
    base = coeffs[0] - coeffs[1]
    shifted_kernel = slope * kernel - eye
    before = jnp.zeros((obs, obs), F32)
    current = slope * eye
    summed = coeffs[1] * current
    for k in range(1, DEGREE):
        sign = -1.0 if k % 2 else 1.0
        if k == 1:
            product = slope * shifted_kernel
        else:
            product = dot_full(shifted_kernel, current)
        following = 2.0 * product - before + (2.0 * sign) * slope * eye
        summed = summed + coeffs[k + 1] * following
        base = base - sign * coeffs[k + 1]
        before, current = current, following
    middle = summed * g_row * g_col
    row = jnp.broadcast_to(weighted, (8, obs))
    for _ in range(2):
        row = base * row + dot_full(dot_full(row, gram), middle)
    row = factor * row[0:1, :]
    root = jnp.sqrt(inflation)
    own = jnp.concatenate([observed(block) for block in blocks], axis=0) - y_mean
    weights_ref[...] = dot_full(own, root * middle) + row
    scale_ref[...] = jnp.broadcast_to(root * base, scale_ref.shape)


def make_weights(sums, target, variance, mean, gram, blocks, each, obs, parts):
    vmem = pl.BlockSpec(memory_space=pltpu.VMEM)
    own = sum(block.shape[1] for block in blocks)
    total = parts * own
    tails = obs // LANES
    slabs, specs = [], []
    for block in blocks:
        for k in range(tails):
            slabs.append(block)
            specs.append(pl.BlockSpec((1, block.shape[1], LANES), lambda i, k=k: (each + k, 0, 0)))
    return pl.pallas_call(
        functools.partial(weights_body, count=len(blocks), obs=obs, total=total),
        grid=(1,),
        in_specs=[vmem] * 5 + specs,
        out_specs=[vmem] * 2,
        out_shape=[
            jax.ShapeDtypeStruct((own, obs), F32),
            jax.ShapeDtypeStruct((8, LANES), F32),
        ],
        compiler_params=params(),
        cost_estimate=pl.CostEstimate(
            flops=10_000_000, bytes_accessed=2_000_000, transcendentals=0
        ),
        name="weights",
    )(sums, target, variance, mean, gram, *slabs)


def segments(begin, end, units, parts, rows):
    found, slot = [], 0
    for count, base in owned_runs(units, parts, rows):
        lo, hi = max(begin, slot), min(end, slot + count)
        if lo < hi:
            found.append((lo - begin, hi - lo, base + lo - slot, count))
        slot += count
    return found


def update_body(
    tiles_ref, owner_ref, scale_ref, weights_ref, *refs, chunks, bounds, units, parts, rows, obs
):
    states = refs[:chunks]
    pieces = refs[chunks : chunks + len(bounds)]
    out_ref, gathered, means, split_w, turned = refs[-5:]
    members = weights_ref.shape[0]

    @pl.when(pl.program_id(0) == 0)
    def _():
        high, low = split2(weights_ref[...])
        split_w[:members] = high
        split_w[members:] = low
        for index, (begin, end) in enumerate(bounds):
            owner = owner_ref[index]
            piece = pieces[index]
            tail = (end - begin) * obs
            for slot, count, base, stride in segments(begin, end, units, parts, rows):
                for j in range(slot, slot + count):
                    unit = base + owner * stride + j - slot
                    gathered[unit] = piece[j * obs : (j + 1) * obs, :]
                    means[unit] = jnp.broadcast_to(
                        piece[tail + j : tail + j + 1, :], (8, LANES)
                    )

    tile = tiles_ref[pl.program_id(0)]
    scale = scale_ref[0:1, :]
    high = split_w[:members]
    both = split_w[...]
    for row in range(0, rows, 2):
        unit = tile * rows + row
        c = [gathered[unit + k] for k in range(2)]
        c_high, c_low = split2(jnp.concatenate(c, axis=1))
        part = dot(both, c_high)
        product = (part[:members] + part[members:]) + dot(high, c_low)
        for k in range(2):
            x = jnp.concatenate([ref[0, row + k] for ref in states], axis=0)
            turned[pl.ds(row + k, members, stride=rows), :] = (
                product[:, k * LANES : (k + 1) * LANES]
                + scale * x
                + (1.0 - scale) * means[unit + k, 0:1, :]
            )
    out_ref[:, 0, :, :] = turned[...].reshape(members, rows, LANES)


def update(tiles, scale, weights, states, pieces, owners, bounds, rows, width, obs, parts, into):
    members = weights.shape[0]
    halves = width // LANES
    units = FIELDS * rows * halves
    views = [s.reshape(FIELDS * halves, rows, s.shape[1], LANES) for s in states]
    vmem = pl.BlockSpec(memory_space=pltpu.VMEM)
    extra = [] if into is None else [into]
    body = functools.partial(
        update_body, chunks=len(states), bounds=bounds, units=units, parts=parts, rows=rows, obs=obs
    )
    operands = [scale, weights, *views, *pieces, *extra]
    return pl.pallas_call(
        body,
        grid_spec=pltpu.PrefetchScalarGridSpec(
            num_scalar_prefetch=2,
            grid=(tiles.shape[0],),
            in_specs=[
                pl.BlockSpec(scale.shape, lambda i, t, o: (0, 0)),
                pl.BlockSpec(weights.shape, lambda i, t, o: (0, 0)),
            ]
            + [
                pl.BlockSpec((1, rows, members, LANES), lambda i, t, o: (t[i], 0, 0, 0))
                for v in views
            ]
            + [pl.BlockSpec(piece.shape, lambda i, t, o: (0, 0)) for piece in pieces]
            + [pl.BlockSpec(memory_space=pl.ANY)] * len(extra),
            out_specs=pl.BlockSpec(
                (members, 1, rows, LANES), lambda i, t, o: (0, t[i] // halves, 0, t[i] % halves)
            ),
            scratch_shapes=[
                pltpu.VMEM((units, obs, LANES), F32),
                pltpu.VMEM((units, 8, LANES), F32),
                pltpu.VMEM((2 * members, obs), BF16),
                pltpu.VMEM((members * rows, LANES), F32),
            ],
        ),
        out_shape=jax.ShapeDtypeStruct((members, FIELDS, rows, width), F32),
        input_output_aliases={} if into is None else {2 + len(operands) - 1: 0},
        compiler_params=params(),
        cost_estimate=pl.CostEstimate(
            flops=10_000_000, bytes_accessed=20_000_000, transcendentals=0
        ),
        name="update" if into is None else "finish",
    )(tiles, owners, *operands)


def chunk_plan(members):
    unit = members // 16
    if unit % 8:
        size = members // CHUNKS
        return [(size * i, size) for i in range(CHUNKS)]
    shares = [(0, 2), (2, 3), (5, 3), (8, 3), (11, 3), (14, 2)]
    return [(unit * begin, unit * size) for begin, size in shares]


def step(ensemble, obs_cells, region_tile, obs_values, obs_error):
    members, _, rows, width = ensemble.shape
    parts = lax.axis_size("mem")
    tiles = lax.axis_size("tile")
    obs = obs_cells.shape[1]
    halves = width // LANES
    units = FIELDS * rows * halves
    each = units // parts
    plan = chunk_plan(members)
    order = sorted(range(len(plan)), key=lambda chunk: plan[chunk])
    up = [(i, (i + 1) % tiles) for i in range(tiles)]
    down = [((i + 1) % tiles, i) for i in range(tiles)]

    def swap(x, p):
        return lax.ppermute(x, "mem", [(i, i ^ p) for i in range(parts)])

    me = jnp.reshape(lax.axis_index("mem"), (1,)).astype(jnp.int32)
    flat = ensemble.reshape(members * FIELDS * rows, width)

    chosen = (region_tile == lax.axis_index("tile"))[:, None]
    obs_index = jnp.sum(jnp.where(chosen, obs_cells, 0), axis=0)
    target = jnp.sum(jnp.where(chosen, obs_values, 0.0), axis=0, keepdims=True)
    variance = jnp.sum(jnp.where(chosen, obs_error, 0.0), axis=0, keepdims=True)
    cells = lax.broadcasted_iota(jnp.int32, (FIELDS * rows, width, obs), 0) * width
    cells = cells + lax.broadcasted_iota(jnp.int32, (FIELDS * rows, width, obs), 1)
    onehot = (cells == obs_index[None, None, :]).astype(BF16)

    pairs = spread(flat, plan[:FIRST], rows, width, SPREAD_VMEM_MIB)
    pairs += spread(flat, plan[FIRST:], rows, width, REST_VMEM_MIB)

    def halo(chunk):
        top, bot = pairs[chunk]
        prev = lax.ppermute(bot, "tile", up)
        return prev, top, bot, lax.ppermute(top, "tile", down)

    blocks, mine, state = [], [], None
    for chunk, (begin, size) in enumerate(plan):
        prev, top, bot, nxt = halo(chunk)
        state, *sends = forecast_chunk(
            me, prev, top, bot, nxt, onehot, state, begin, size, members, rows, width, parts, obs
        )
        mine.append(sends[0])
        blocks.append(sends[0])
        for p in reversed(range(1, parts)):
            blocks.append(swap(sends[p], p))

    late = len(blocks) - parts
    early = early_covariance(blocks[:late], each, obs)
    c_first, c_second, sums, y_mean, gram = late_covariance(
        target, variance, early, blocks[late:], each, obs, parts * (members - plan[-1][1])
    )
    first = (each + 1) // 2
    bounds = [(0, first), (first, each)]
    sums = lax.psum(jnp.sum(sums, axis=1)[None, :], "tile")
    weights, scale = make_weights(
        sums, target, variance, y_mean, gram, [mine[chunk] for chunk in order], each, obs, parts
    )
    args = (scale, weights, [state])
    sizes_of = (rows, width, obs, parts)
    if parts == 4 and each == rows + rows // 2:
        x_first, y_second = swap(c_first, 1), swap(c_second, 2)
        x_second, y_first = swap(c_second, 1), swap(c_first, 2)
        far_first, far_second = swap(x_first, 2), swap(y_second, 1)
        own, x, y, far = me, me ^ 1, me ^ 2, me ^ 3
        done = update(
            jnp.concatenate([own, x, y, parts + own // 2]),
            *args,
            [c_first, c_second, x_first, x_second, y_first, y_second],
            jnp.concatenate([own, own, x, x, y, y]),
            bounds * 3,
            *sizes_of,
            None,
        )
        return update(
            jnp.concatenate([far, parts + far // 2]),
            *args,
            [far_first, far_second, y_second],
            jnp.concatenate([far, far, y]),
            bounds + bounds[1:],
            *sizes_of,
            done,
        )
    pieces, owners = [], []
    for p in range(parts):
        for piece in (c_first, c_second):
            pieces.append(swap(piece, p) if p else piece)
            owners.append(me ^ p)
    return update(
        jnp.arange(FIELDS * halves, dtype=jnp.int32),
        *args,
        pieces,
        jnp.concatenate(owners),
        bounds * parts,
        *sizes_of,
        None,
    )


def solution(mesh):
    in_specs = (P("mem", None, "tile", None), P(), P(), P(), P())
    out_specs = P("mem", None, "tile", None)
    return jax.shard_map(step, mesh=mesh, in_specs=in_specs, out_specs=out_specs, check_vma=False)
```

profile of v0, /device:TPU:0, one launch (start us, length us, event | category | flops | bytes accessed | tf_op | source)
XLA Modules:
  0.0 236.3 jit_solution(15035541535279210284)
XLA Ops:
  0.0 2.9 %spread.2 = (f32[12,32,256]{2,1,0:T(8,128)}, f32[12,32,256]{2,1,0:T(8,128)}, f32[12,48,256]{2,1,0:T(8,128)}, f32[12,48,256]{2,1,0:T(8,128)}) custom-call(f32[6144,256]{1,0:T(8,128)} %bitcast.6), custom_call_target="tpu_custom_call" | custom-call | tf_op jit(solution)/shard_map/spread/pallas_call | solution.py:85
  2.9 0.5 collective-permute-start.5
  3.4 4.1 %collective-permute-start.6 = (f32[12,48,256]{2,1,0:T(8,128)}, f32[12,48,256]{2,1,0:T(8,128)}, u32[]{:S(2)}, u32[]{:S(2)}) collective-permute-start(f32[12,48,256]{2,1,0:T(8,128)} %get-tuple-element.64.top_ref), channel_id=1, source_target_pairs={{1,0},{2,1},{3,2},{4,3},{5,4},{6,5},{7,6},{0,7},{9,8},{10,9},{11,1... | collective-permute-start | bytes 1769480 | tf_op jit(solution)/shard_map/ppermute | solution.py:622
  7.5 2.8 %copy-done = f32[256,3,8,256]{3,2,1,0:T(8,128)S(1)} copy-done((f32[256,3,8,256]{3,2,1,0:T(8,128)S(1)}, f32[256,3,8,256]{3,2,1,0:T(8,128)}, u32[]{:S(2)}) %copy-start) | copy-done | bytes 6291480
  10.3 2.0 spread.3
  12.7 3.3 %collective-permute-start.1 = (f32[12,32,256]{2,1,0:T(8,128)S(1)}, f32[12,32,256]{2,1,0:T(8,128)S(1)}, u32[]{:S(2)}, u32[]{:S(2)}) collective-permute-start(f32[12,32,256]{2,1,0:T(8,128)S(1)} %copy-done.11), channel_id=1, source_target_pairs={{1,0},{2,1},{3,2},{4,3},{5,4},{6,5},{7,6},{0,7},{9,8},{10,9},{11,1... | collective-permute-start | bytes 1179656 | tf_op jit(solution)/shard_map/ppermute | solution.py:622
  16.0 20.3 %collective-permute-done.prev_ref = f32[12,32,256]{2,1,0:T(8,128)S(1)} collective-permute-done((f32[12,32,256]{2,1,0:T(8,128)S(1)}, f32[12,32,256]{2,1,0:T(8,128)S(1)}, u32[]{:S(2)}, u32[]{:S(2)}) %collective-permute-start) | collective-permute-done | bytes 393248 | tf_op jit(solution)/shard_map/ppermute | solution.py:621
  36.3 0.7 copy-done.15
  37.1 0.7 copy-done.17
  38.3 3.0 %collective-permute-start.16 = (f32[12,48,256]{2,1,0:T(8,128)S(1)}, f32[12,48,256]{2,1,0:T(8,128)}, u32[]{:S(2)}, u32[]{:S(2)}) collective-permute-start(f32[12,48,256]{2,1,0:T(8,128)S(1)} %get-tuple-element.78.top_ref), channel_id=1, source_target_pairs={{1,0},{2,1},{3,2},{4,3},{5,4},{6,5},{7,6},{0,7},{9,8},{10,9},{11,1... | collective-permute-start | bytes 1769480 | tf_op jit(solution)/shard_map/ppermute | solution.py:622
  41.4 3.5 %collective-permute-start.21 = (f32[12,48,256]{2,1,0:T(8,128)S(1)}, f32[12,48,256]{2,1,0:T(8,128)}, u32[]{:S(2)}, u32[]{:S(2)}) collective-permute-start(f32[12,48,256]{2,1,0:T(8,128)S(1)} %get-tuple-element.85.top_ref), channel_id=1, source_target_pairs={{1,0},{2,1},{3,2},{4,3},{5,4},{6,5},{7,6},{0,7},{9,8},{10,9},{11,1... | collective-permute-start | bytes 1769480 | tf_op jit(solution)/shard_map/ppermute | solution.py:622
  45.0 5.2 %collective-permute-done.11.next_ref = f32[12,48,256]{2,1,0:T(8,128)} collective-permute-done((f32[12,48,256]{2,1,0:T(8,128)S(1)}, f32[12,48,256]{2,1,0:T(8,128)}, u32[]{:S(2)}, u32[]{:S(2)}) %collective-permute-start.11) | collective-permute-done | bytes 589856 | tf_op jit(solution)/shard_map/ppermute | solution.py:622
  50.2 5.1 %collective-permute-done.15.prev_ref = f32[12,48,256]{2,1,0:T(8,128)} collective-permute-done((f32[12,48,256]{2,1,0:T(8,128)S(1)}, f32[12,48,256]{2,1,0:T(8,128)}, u32[]{:S(2)}, u32[]{:S(2)}) %collective-permute-start.15) | collective-permute-done | bytes 589856 | tf_op jit(solution)/shard_map/ppermute | solution.py:621
  55.3 0.9 fusion.onehot_ref
  56.3 1.0 copy-done.12
  57.3 1.0 copy-done.14
  58.3 1.0 copy-done.16
  59.3 1.0 copy-done.18
  60.3 4.0 %forecast.6 = (f32[48,2048,128]{2,1,0:T(8,128)}, f32[14,32,128]{2,1,0:T(8,128)S(1)}, f32[14,32,128]{2,1,0:T(8,128)S(1)}, f32[14,32,128]{2,1,0:T(8,128)S(1)}, f32[14,32,128]{2,1,0:T(8,128)S(1)}) custom-call(s32[1]{0:T(128)} %bitcast.me_ref, f32[12,32,256]{2,1,0:T(8,128)S(1)} %copy-done.16, f32[12,32,256]{2,1,0:T(8,128)S(1)} %copy-done.12, ...), custom_call_target="tpu_custom_call" | custom-call | flops 50000000 | bytes 8000000 | tf_op jit(solution)/shard_map/forecast/pallas_call | solution.py:234
  64.3 3.0 %collective-permute-start.2 = (f32[14,32,128]{2,1,0:T(8,128)S(1)}, f32[14,32,128]{2,1,0:T(8,128)S(1)}, u32[]{:S(2)}, u32[]{:S(2)}) collective-permute-start(f32[14,32,128]{2,1,0:T(8,128)S(1)} %get-tuple-element.60), channel_id=1, source_target_pairs={{0,24},{8,16},{16,8},{24,0},{1,25},{9,17},{17,9},{25,1},{2,26},{10... | collective-permute-start | bytes 688136 | tf_op jit(solution)/shard_map/ppermute | solution.py:603
  67.3 0.7 collective-permute-done.20.prev_ref
  68.0 2.0 collective-permute-start.3
  70.0 3.9 %collective-permute-done.21.next_ref = f32[12,48,256]{2,1,0:T(8,128)} collective-permute-done((f32[12,48,256]{2,1,0:T(8,128)S(1)}, f32[12,48,256]{2,1,0:T(8,128)}, u32[]{:S(2)}, u32[]{:S(2)}) %collective-permute-start.21) | collective-permute-done | bytes 589856 | tf_op jit(solution)/shard_map/ppermute | solution.py:622
  73.9 2.0 collective-permute-start.4
  75.9 1.1 copy-done.5
  77.0 1.1 copy-done.6
  78.1 6.4 %forecast.7 = (f32[48,2048,128]{2,1,0:T(8,128)}, f32[14,48,128]{2,1,0:T(8,128)S(1)}, f32[14,48,128]{2,1,0:T(8,128)S(1)}, f32[14,48,128]{2,1,0:T(8,128)S(1)}, f32[14,48,128]{2,1,0:T(8,128)S(1)}) custom-call(s32[1]{0:T(128)} %bitcast.me_ref, f32[12,48,256]{2,1,0:T(8,128)} %collective-permute-done.5.prev_ref, ...), custom_call_target="tpu_custom_call", output_to_operand_aliasing={{0}: (6, {})} | custom-call | flops 50000000 | bytes 8000000 | tf_op jit(solution)/shard_map/forecast/pallas_call | solution.py:234
  84.5 6.6 %forecast.8 = (f32[48,2048,128]{2,1,0:T(8,128)}, f32[14,48,128]{2,1,0:T(8,128)S(1)}, f32[14,48,128]{2,1,0:T(8,128)S(1)}, f32[14,48,128]{2,1,0:T(8,128)S(1)}, f32[14,48,128]{2,1,0:T(8,128)S(1)}) custom-call(s32[1]{0:T(128)} %bitcast.me_ref, f32[12,48,256]{2,1,0:T(8,128)} %collective-permute-done.10.prev_ref, ...), custom_call_target="tpu_custom_call", output_to_operand_aliasing={{0}: (6, {})} | custom-call | flops 50000000 | bytes 8000000 | tf_op jit(solution)/shard_map/forecast/pallas_call | solution.py:234
  91.1 6.4 %forecast.9 = (f32[48,2048,128]{2,1,0:T(8,128)}, f32[14,48,128]{2,1,0:T(8,128)S(1)}, f32[14,48,128]{2,1,0:T(8,128)S(1)}, f32[14,48,128]{2,1,0:T(8,128)S(1)}, f32[14,48,128]{2,1,0:T(8,128)S(1)}) custom-call(s32[1]{0:T(128)} %bitcast.me_ref, f32[12,48,256]{2,1,0:T(8,128)} %collective-permute-done.15.prev_ref, ...), custom_call_target="tpu_custom_call", output_to_operand_aliasing={{0}: (6, {})} | custom-call | flops 50000000 | bytes 8000000 | tf_op jit(solution)/shard_map/forecast/pallas_call | solution.py:234
  97.5 6.4 %forecast.10 = (f32[48,2048,128]{2,1,0:T(8,128)}, f32[14,48,128]{2,1,0:T(8,128)S(1)}, f32[14,48,128]{2,1,0:T(8,128)S(1)}, f32[14,48,128]{2,1,0:T(8,128)S(1)}, f32[14,48,128]{2,1,0:T(8,128)S(1)}) custom-call(s32[1]{0:T(128)} %bitcast.me_ref, f32[12,48,256]{2,1,0:T(8,128)} %collective-permute-done.20.prev_ref, ...), custom_call_target="tpu_custom_call", output_to_operand_aliasing={{0}: (6, {})} | custom-call | flops 50000000 | bytes 8000000 | tf_op jit(solution)/shard_map/forecast/pallas_call | solution.py:234
  104.0 1.6 collective-permute-start.22
  105.7 1.9 collective-permute-start.24
  107.6 1.5 collective-permute-start.17
  109.2 6.7 %collective-permute-done.22.refs_17_ = f32[14,48,128]{2,1,0:T(8,128)S(1)} collective-permute-done((f32[14,48,128]{2,1,0:T(8,128)S(1)}, f32[14,48,128]{2,1,0:T(8,128)S(1)}, u32[]{:S(2)}, u32[]{:S(2)}) %collective-permute-start.22) | collective-permute-done | bytes 344096 | tf_op jit(solution)/shard_map/ppermute | solution.py:603
  116.0 7.3 %collective-permute-done.23.refs_18_ = f32[14,48,128]{2,1,0:T(8,128)S(1)} collective-permute-done((f32[14,48,128]{2,1,0:T(8,128)S(1)}, f32[14,48,128]{2,1,0:T(8,128)S(1)}, u32[]{:S(2)}, u32[]{:S(2)}) %collective-permute-start.23) | collective-permute-done | bytes 344096 | tf_op jit(solution)/shard_map/ppermute | solution.py:603
  123.3 1.5 collective-permute-start.12
  124.9 5.8 %collective-permute-done.17.refs_13_ = f32[14,48,128]{2,1,0:T(8,128)S(1)} collective-permute-done((f32[14,48,128]{2,1,0:T(8,128)S(1)}, f32[14,48,128]{2,1,0:T(8,128)S(1)}, u32[]{:S(2)}, u32[]{:S(2)}) %collective-permute-start.17) | collective-permute-done | bytes 344096 | tf_op jit(solution)/shard_map/ppermute | solution.py:603
  130.8 7.3 %collective-permute-done.18.refs_14_ = f32[14,48,128]{2,1,0:T(8,128)S(1)} collective-permute-done((f32[14,48,128]{2,1,0:T(8,128)S(1)}, f32[14,48,128]{2,1,0:T(8,128)S(1)}, u32[]{:S(2)}, u32[]{:S(2)}) %collective-permute-start.18) | collective-permute-done | bytes 344096 | tf_op jit(solution)/shard_map/ppermute | solution.py:603
  138.1 1.5 collective-permute-start.7
  139.6 5.8 %collective-permute-done.12.refs_9_ = f32[14,48,128]{2,1,0:T(8,128)S(1)} collective-permute-done((f32[14,48,128]{2,1,0:T(8,128)S(1)}, f32[14,48,128]{2,1,0:T(8,128)S(1)}, u32[]{:S(2)}, u32[]{:S(2)}) %collective-permute-start.12) | collective-permute-done | bytes 344096 | tf_op jit(solution)/shard_map/ppermute | solution.py:603
  145.6 4.2 %forecast.11 = (f32[48,2048,128]{2,1,0:T(8,128)}, f32[14,32,128]{2,1,0:T(8,128)S(1)}, f32[14,32,128]{2,1,0:T(8,128)S(1)}, f32[14,32,128]{2,1,0:T(8,128)S(1)}, f32[14,32,128]{2,1,0:T(8,128)S(1)}) custom-call(s32[1]{0:T(128)} %bitcast.me_ref, f32[12,32,256]{2,1,0:T(8,128)S(1)} %collective-permute-done.25.prev_ref, ...), custom_call_target="tpu_custom_call", output_to_operand_aliasing={{0}: (6, {})} | custom-call | flops 50000000 | bytes 8000000 | tf_op jit(solution)/shard_map/forecast/pallas_call | solution.py:234
  149.8 3.0 %collective-permute-done.13.refs_10_ = f32[14,48,128]{2,1,0:T(8,128)S(1)} collective-permute-done((f32[14,48,128]{2,1,0:T(8,128)S(1)}, f32[14,48,128]{2,1,0:T(8,128)S(1)}, u32[]{:S(2)}, u32[]{:S(2)}) %collective-permute-start.13) | collective-permute-done | bytes 344096 | tf_op jit(solution)/shard_map/ppermute | solution.py:603
  152.8 1.5 collective-permute-start.27
  154.3 5.9 %collective-permute-done.7.refs_5_ = f32[14,48,128]{2,1,0:T(8,128)S(1)} collective-permute-done((f32[14,48,128]{2,1,0:T(8,128)S(1)}, f32[14,48,128]{2,1,0:T(8,128)S(1)}, u32[]{:S(2)}, u32[]{:S(2)}) %collective-permute-start.7) | collective-permute-done | bytes 344096 | tf_op jit(solution)/shard_map/ppermute | solution.py:603
  160.5 6.6 %collective-permute-done.8.refs_6_ = f32[14,48,128]{2,1,0:T(8,128)S(1)} collective-permute-done((f32[14,48,128]{2,1,0:T(8,128)S(1)}, f32[14,48,128]{2,1,0:T(8,128)S(1)}, u32[]{:S(2)}, u32[]{:S(2)}) %collective-permute-start.8) | collective-permute-done | bytes 344096 | tf_op jit(solution)/shard_map/ppermute | solution.py:603
  167.0 0.7 collective-permute-done.9.refs_7_
  167.7 3.6 %early.1 = (f32[14,256,128]{2,1,0:T(8,128)S(1)}, f32[14,128]{1,0:T(8,128)S(1)}, f32[2,256]{1,0:T(2,128)S(1)}) custom-call(f32[14,32,128]{2,1,0:T(8,128)S(1)} %get-tuple-element.59.refs_0_.refs_1_, f32[14,32,128]{2,1,0:T(8,128)S(1)} %collective-permute-done.2.refs_1_, f32[14,32,128]{2,1,0:T(8,128)S(1)} %collective-permute-done.3.refs_2_, ...), custom_call_target="tpu_custom_call" | custom-call | flops 10000000 | bytes 8000000 | tf_op jit(solution)/shard_map/early/pallas_call | solution.py:311
  171.3 0.8 collective-permute-done.27.refs_1_
  172.1 2.2 collective-permute-done.28.refs_2_
  174.5 1.9 late.1
  176.5 0.7 copy-done.19
  177.2 0.8 collective-permute-start.30
  178.0 1.0 collective-permute-start.32
  179.0 1.3 collective-permute-start.34
  180.3 0.9 collective-permute-start.35
  181.2 16.6 %collective-permute-done.30.refs_3_ = f32[1544,128]{1,0:T(8,128)} collective-permute-done((f32[1544,128]{1,0:T(8,128)S(1)}, f32[1544,128]{1,0:T(8,128)}, u32[]{:S(2)}, u32[]{:S(2)}) %collective-permute-start.30) | collective-permute-done | bytes 790560 | tf_op jit(solution)/shard_map/ppermute | solution.py:603
  197.8 1.1 collective-permute-start.31
  198.9 1.0 collective-permute-start.33
  200.3 15.4 %psum.7.sums_ref = f32[1,2]{1,0:T(1,128)S(1)} all-reduce(f32[1,2]{1,0:T(1,128)S(1)} %bitcast.14), channel_id=1, replica_groups=mesh['mem'=4,'tile'=8] {'tile'}, use_global_device_ids=true, to_apply=%region_4.5 | all-reduce | flops 2 | bytes 16 | tf_op jit(solution)/shard_map/psum | solution.py:642
  215.8 0.9 copy-done.20
  216.7 2.5 %weights.1 = (f32[256,256]{1,0:T(8,128)S(1)}, f32[8,128]{1,0:T(8,128)S(1)}) custom-call(f32[1,2]{1,0:T(1,128)S(1)} %psum.7.sums_ref, f32[1,256]{1,0:T(1,128)S(1)} %bitcast.11, f32[1,256]{1,0:T(1,128)S(1)} %bitcast.9, f32[8,256]{1,0:T(8,128)S(1)} %get-tuple-element.102.mean_ref, f32[256,256]{1,0:T(8,128)S(1)} %copy-done.20, ...), custom_call_target="tpu_custom_call" | custom-call | flops 10000000 | bytes 2000000 | tf_op jit(solution)/shard_map/weights/pallas_call | solution.py:462
  219.2 7.9 %update.1.refs_4_ = f32[256,3,8,256]{3,2,1,0:T(8,128)} custom-call(s32[4]{0:T(128)S(1)} %pad_add_fusion.2.tiles_ref, s32[6]{0:T(128)S(1)} %concatenate.15.owner_ref, f32[8,128]{1,0:T(8,128)S(1)} %get-tuple-element.104.scale_ref, f32[256,256]{1,0:T(8,128)S(1)} %get-tuple-element.105.weights_ref, f32[6,8,2048,128]{3,2,1,0:T(8,128)} %bitcast.12, ...), custom_call_target="tpu_custom_call" | custom-call | flops 10000000 | bytes 20000000 | tf_op jit(solution)/shard_map/update/pallas_call | solution.py:545
  227.1 4.3 %collective-permute-done.31.refs_1_ = f32[1544,128]{1,0:T(8,128)} collective-permute-done((f32[1544,128]{1,0:T(8,128)}, f32[1544,128]{1,0:T(8,128)}, u32[]{:S(2)}, u32[]{:S(2)}) %collective-permute-start.31) | collective-permute-done | bytes 790560 | tf_op jit(solution)/shard_map/ppermute | solution.py:603
  231.4 4.9 %finish.1 = f32[256,3,8,256]{3,2,1,0:T(8,128)} custom-call(s32[2]{0:T(128)S(1)} %pad_add_fusion.tiles_ref, s32[3]{0:T(128)S(1)} %pad_add_fusion.1.owner_ref, f32[8,128]{1,0:T(8,128)S(1)} %get-tuple-element.104.scale_ref, f32[256,256]{1,0:T(8,128)S(1)} %get-tuple-element.105.weights_ref, ...), custom_call_target="tpu_custom_call", output_to_operand_aliasing={{}: (8, {})} | custom-call | flops 10000000 | bytes 20000000 | tf_op jit(solution)/shard_map/finish/pallas_call | solution.py:545
  (82 shorter events, 2.7 us)
Async XLA Ops:
  0.0 44.9 %copy-start.24 = (s32[8]{0:T(128)S(1)}, s32[8]{0:T(128)}, u32[]{:S(2)}) copy-start(s32[8]{0:T(128)} %param.7) | copy-start | bytes 100
  0.0 44.9 %copy-start.23 = (s32[8,256]{1,0:T(8,128)S(1)}, s32[8,256]{1,0:T(8,128)}, u32[]{:S(2)}) copy-start(s32[8,256]{1,0:T(8,128)} %param.6) | copy-start | bytes 24580
  2.9 35.4 %collective-permute-start.5 = (f32[12,48,256]{2,1,0:T(8,128)}, f32[12,48,256]{2,1,0:T(8,128)}, u32[]{:S(2)}, u32[]{:S(2)}) collective-permute-start(f32[12,48,256]{2,1,0:T(8,128)} %get-tuple-element.63.bot_ref), channel_id=1, source_target_pairs={{0,1},{1,2},{2,3},{3,4},{4,5},{5,6},{6,7},{7,0},{8,9},{9,10},{10,1... | collective-permute-start | bytes 1769480 | tf_op jit(solution)/shard_map/ppermute | solution.py:621
  3.4 37.9 %collective-permute-start.6 = (f32[12,48,256]{2,1,0:T(8,128)}, f32[12,48,256]{2,1,0:T(8,128)}, u32[]{:S(2)}, u32[]{:S(2)}) collective-permute-start(f32[12,48,256]{2,1,0:T(8,128)} %get-tuple-element.64.top_ref), channel_id=1, source_target_pairs={{1,0},{2,1},{3,2},{4,3},{5,4},{6,5},{7,6},{0,7},{9,8},{10,9},{11,1... | collective-permute-start | bytes 1769480 | tf_op jit(solution)/shard_map/ppermute | solution.py:622
  7.5 2.8 %copy-start = (f32[256,3,8,256]{3,2,1,0:T(8,128)S(1)}, f32[256,3,8,256]{3,2,1,0:T(8,128)}, u32[]{:S(2)}) copy-start(f32[256,3,8,256]{3,2,1,0:T(8,128)} %param.5) | copy-start | bytes 18874372
  10.3 2.1 copy-start.13
  10.3 2.4 %copy-start.11 = (f32[12,32,256]{2,1,0:T(8,128)S(1)}, f32[12,32,256]{2,1,0:T(8,128)}, u32[]{:S(2)}) copy-start(f32[12,32,256]{2,1,0:T(8,128)} %get-tuple-element.58.top_ref) | copy-start | bytes 1179652
  12.3 24.8 %copy-start.9 = (f32[12,32,256]{2,1,0:T(8,128)}, f32[12,32,256]{2,1,0:T(8,128)S(1)}, u32[]{:S(2)}) copy-start(f32[12,32,256]{2,1,0:T(8,128)S(1)} %get-tuple-element.94.bot_ref) | copy-start | bytes 1179652
  12.3 44.0 %copy-start.7 = (f32[12,48,256]{2,1,0:T(8,128)}, f32[12,48,256]{2,1,0:T(8,128)S(1)}, u32[]{:S(2)}) copy-start(f32[12,48,256]{2,1,0:T(8,128)S(1)} %get-tuple-element.71.top_ref) | copy-start | bytes 1769476
  12.3 63.6 %copy-start.1 = (f32[12,48,256]{2,1,0:T(8,128)}, f32[12,48,256]{2,1,0:T(8,128)S(1)}, u32[]{:S(2)}) copy-start(f32[12,48,256]{2,1,0:T(8,128)S(1)} %get-tuple-element.78.top_ref) | copy-start | bytes 1769476
  12.3 72.2 %copy-start.3 = (f32[12,48,256]{2,1,0:T(8,128)}, f32[12,48,256]{2,1,0:T(8,128)S(1)}, u32[]{:S(2)}) copy-start(f32[12,48,256]{2,1,0:T(8,128)S(1)} %get-tuple-element.77.bot_ref) | copy-start | bytes 1769476
  12.3 29.0 %collective-permute-start.10 = (f32[12,48,256]{2,1,0:T(8,128)}, f32[12,48,256]{2,1,0:T(8,128)}, u32[]{:S(2)}, u32[]{:S(2)}) collective-permute-start(f32[12,48,256]{2,1,0:T(8,128)} %get-tuple-element.70.bot_ref), channel_id=1, source_target_pairs={{0,1},{1,2},{2,3},{3,4},{4,5},{5,6},{6,7},{7,0},{8,9},{9,10},{10,1... | collective-permute-start | bytes 1769480 | tf_op jit(solution)/shard_map/ppermute | solution.py:621
  12.4 23.9 %collective-permute-start = (f32[12,32,256]{2,1,0:T(8,128)S(1)}, f32[12,32,256]{2,1,0:T(8,128)S(1)}, u32[]{:S(2)}, u32[]{:S(2)}) collective-permute-start(f32[12,32,256]{2,1,0:T(8,128)S(1)} %copy-done.13), channel_id=1, source_target_pairs={{0,1},{1,2},{2,3},{3,4},{4,5},{5,6},{6,7},{7,0},{8,9},{9,10},{10,1... | collective-permute-start | bytes 1179656 | tf_op jit(solution)/shard_map/ppermute | solution.py:621
  12.7 24.3 %collective-permute-start.1 = (f32[12,32,256]{2,1,0:T(8,128)S(1)}, f32[12,32,256]{2,1,0:T(8,128)S(1)}, u32[]{:S(2)}, u32[]{:S(2)}) collective-permute-start(f32[12,32,256]{2,1,0:T(8,128)S(1)} %copy-done.11), channel_id=1, source_target_pairs={{1,0},{2,1},{3,2},{4,3},{5,4},{6,5},{7,6},{0,7},{9,8},{10,9},{11,1... | collective-permute-start | bytes 1179656 | tf_op jit(solution)/shard_map/ppermute | solution.py:622
  36.3 0.7 copy-start.15
  37.0 13.1 %collective-permute-start.11 = (f32[12,48,256]{2,1,0:T(8,128)S(1)}, f32[12,48,256]{2,1,0:T(8,128)}, u32[]{:S(2)}, u32[]{:S(2)}) collective-permute-start(f32[12,48,256]{2,1,0:T(8,128)S(1)} %get-tuple-element.71.top_ref), channel_id=1, source_target_pairs={{1,0},{2,1},{3,2},{4,3},{5,4},{6,5},{7,6},{0,7},{9,8},{10,9},{11,1... | collective-permute-start | bytes 1769480 | tf_op jit(solution)/shard_map/ppermute | solution.py:622
  37.0 0.7 copy-start.17
  37.8 17.5 %collective-permute-start.15 = (f32[12,48,256]{2,1,0:T(8,128)S(1)}, f32[12,48,256]{2,1,0:T(8,128)}, u32[]{:S(2)}, u32[]{:S(2)}) collective-permute-start(f32[12,48,256]{2,1,0:T(8,128)S(1)} %get-tuple-element.77.bot_ref), channel_id=1, source_target_pairs={{0,1},{1,2},{2,3},{3,4},{4,5},{5,6},{6,7},{7,0},{8,9},{9,10},{10,1... | collective-permute-start | bytes 1769480 | tf_op jit(solution)/shard_map/ppermute | solution.py:621
  38.3 26.0 %collective-permute-start.16 = (f32[12,48,256]{2,1,0:T(8,128)S(1)}, f32[12,48,256]{2,1,0:T(8,128)}, u32[]{:S(2)}, u32[]{:S(2)}) collective-permute-start(f32[12,48,256]{2,1,0:T(8,128)S(1)} %get-tuple-element.78.top_ref), channel_id=1, source_target_pairs={{1,0},{2,1},{3,2},{4,3},{5,4},{6,5},{7,6},{0,7},{9,8},{10,9},{11,1... | collective-permute-start | bytes 1769480 | tf_op jit(solution)/shard_map/ppermute | solution.py:622
  41.3 26.6 %collective-permute-start.20 = (f32[12,48,256]{2,1,0:T(8,128)S(1)}, f32[12,48,256]{2,1,0:T(8,128)}, u32[]{:S(2)}, u32[]{:S(2)}) collective-permute-start(f32[12,48,256]{2,1,0:T(8,128)S(1)} %get-tuple-element.84.bot_ref), channel_id=1, source_target_pairs={{0,1},{1,2},{2,3},{3,4},{4,5},{5,6},{6,7},{7,0},{8,9},{9,10},{10,1... | collective-permute-start | bytes 1769480 | tf_op jit(solution)/shard_map/ppermute | solution.py:621
  41.4 32.6 %collective-permute-start.21 = (f32[12,48,256]{2,1,0:T(8,128)S(1)}, f32[12,48,256]{2,1,0:T(8,128)}, u32[]{:S(2)}, u32[]{:S(2)}) collective-permute-start(f32[12,48,256]{2,1,0:T(8,128)S(1)} %get-tuple-element.85.top_ref), channel_id=1, source_target_pairs={{1,0},{2,1},{3,2},{4,3},{5,4},{6,5},{7,6},{0,7},{9,8},{10,9},{11,1... | collective-permute-start | bytes 1769480 | tf_op jit(solution)/shard_map/ppermute | solution.py:622
  50.2 53.8 %collective-permute-start.25 = (f32[12,32,256]{2,1,0:T(8,128)}, f32[12,32,256]{2,1,0:T(8,128)S(1)}, u32[]{:S(2)}, u32[]{:S(2)}) collective-permute-start(f32[12,32,256]{2,1,0:T(8,128)} %copy-done.9), channel_id=1, source_target_pairs={{0,1},{1,2},{2,3},{3,4},{4,5},{5,6},{6,7},{7,0},{8,9},{9,10},{10,1... | collective-permute-start | bytes 1179656 | tf_op jit(solution)/shard_map/ppermute | solution.py:621
  55.3 50.2 %collective-permute-start.26 = (f32[12,32,256]{2,1,0:T(8,128)S(1)}, f32[12,32,256]{2,1,0:T(8,128)S(1)}, u32[]{:S(2)}, u32[]{:S(2)}) collective-permute-start(f32[12,32,256]{2,1,0:T(8,128)S(1)} %get-tuple-element.95.top_ref), channel_id=1, source_target_pairs={{1,0},{2,1},{3,2},{4,3},{5,4},{6,5},{7,6},{0,7},{9,8},{10,9},{11,1... | collective-permute-start | bytes 1179656 | tf_op jit(solution)/shard_map/ppermute | solution.py:622
  56.3 1.0 copy-start.12
  57.3 1.0 copy-start.14
  58.3 1.0 copy-start.16
  59.3 1.0 copy-start.18
  64.3 41.4 %collective-permute-start.2 = (f32[14,32,128]{2,1,0:T(8,128)S(1)}, f32[14,32,128]{2,1,0:T(8,128)S(1)}, u32[]{:S(2)}, u32[]{:S(2)}) collective-permute-start(f32[14,32,128]{2,1,0:T(8,128)S(1)} %get-tuple-element.60), channel_id=1, source_target_pairs={{0,24},{8,16},{16,8},{24,0},{1,25},{9,17},{17,9},{25,1},{2,26},{10... | collective-permute-start | bytes 688136 | tf_op jit(solution)/shard_map/ppermute | solution.py:603
  68.0 39.6 %collective-permute-start.3 = (f32[14,32,128]{2,1,0:T(8,128)S(1)}, f32[14,32,128]{2,1,0:T(8,128)S(1)}, u32[]{:S(2)}, u32[]{:S(2)}) collective-permute-start(f32[14,32,128]{2,1,0:T(8,128)S(1)} %get-tuple-element.61), channel_id=1, source_target_pairs={{0,16},{8,24},{16,0},{24,8},{1,17},{9,25},{17,1},{25,9},{2,18},{10... | collective-permute-start | bytes 688136 | tf_op jit(solution)/shard_map/ppermute | solution.py:603
  73.9 35.1 %collective-permute-start.4 = (f32[14,32,128]{2,1,0:T(8,128)S(1)}, f32[14,32,128]{2,1,0:T(8,128)S(1)}, u32[]{:S(2)}, u32[]{:S(2)}) collective-permute-start(f32[14,32,128]{2,1,0:T(8,128)S(1)} %get-tuple-element.62), channel_id=1, source_target_pairs={{0,8},{8,0},{16,24},{24,16},{1,9},{9,1},{17,25},{25,17},{2,10},{10... | collective-permute-start | bytes 688136 | tf_op jit(solution)/shard_map/ppermute | solution.py:603
  75.9 1.1 copy-start.5
  77.0 1.1 copy-start.6
  78.1 6.5 %copy-start.8 = (f32[12,48,256]{2,1,0:T(8,128)S(1)}, f32[12,48,256]{2,1,0:T(8,128)}, u32[]{:S(2)}) copy-start(f32[12,48,256]{2,1,0:T(8,128)} %copy-done.7) | copy-start | bytes 1769476
  84.5 6.6 %copy-start.2 = (f32[12,48,256]{2,1,0:T(8,128)S(1)}, f32[12,48,256]{2,1,0:T(8,128)}, u32[]{:S(2)}) copy-start(f32[12,48,256]{2,1,0:T(8,128)} %copy-done.1) | copy-start | bytes 1769476
  84.5 6.6 %copy-start.4 = (f32[12,48,256]{2,1,0:T(8,128)S(1)}, f32[12,48,256]{2,1,0:T(8,128)}, u32[]{:S(2)}) copy-start(f32[12,48,256]{2,1,0:T(8,128)} %copy-done.3) | copy-start | bytes 1769476
  97.5 48.0 %copy-start.10 = (f32[12,32,256]{2,1,0:T(8,128)S(1)}, f32[12,32,256]{2,1,0:T(8,128)}, u32[]{:S(2)}) copy-start(f32[12,32,256]{2,1,0:T(8,128)} %copy-done.9) | copy-start | bytes 1179652
  104.0 11.9 %collective-permute-start.22 = (f32[14,48,128]{2,1,0:T(8,128)S(1)}, f32[14,48,128]{2,1,0:T(8,128)S(1)}, u32[]{:S(2)}, u32[]{:S(2)}) collective-permute-start(f32[14,48,128]{2,1,0:T(8,128)S(1)} %get-tuple-element.88), channel_id=1, source_target_pairs={{0,24},{8,16},{16,8},{24,0},{1,25},{9,17},{17,9},{25,1},{2,26},{10... | collective-permute-start | bytes 1032200 | tf_op jit(solution)/shard_map/ppermute | solution.py:603
  105.5 17.8 %collective-permute-start.23 = (f32[14,48,128]{2,1,0:T(8,128)S(1)}, f32[14,48,128]{2,1,0:T(8,128)S(1)}, u32[]{:S(2)}, u32[]{:S(2)}) collective-permute-start(f32[14,48,128]{2,1,0:T(8,128)S(1)} %get-tuple-element.89), channel_id=1, source_target_pairs={{0,16},{8,24},{16,0},{24,8},{1,17},{9,25},{17,1},{25,9},{2,18},{10... | collective-permute-start | bytes 1032200 | tf_op jit(solution)/shard_map/ppermute | solution.py:603
  105.7 19.1 %collective-permute-start.24 = (f32[14,48,128]{2,1,0:T(8,128)S(1)}, f32[14,48,128]{2,1,0:T(8,128)S(1)}, u32[]{:S(2)}, u32[]{:S(2)}) collective-permute-start(f32[14,48,128]{2,1,0:T(8,128)S(1)} %get-tuple-element.90), channel_id=1, source_target_pairs={{0,8},{8,0},{16,24},{24,16},{1,9},{9,1},{17,25},{25,17},{2,10},{10... | collective-permute-start | bytes 1032200 | tf_op jit(solution)/shard_map/ppermute | solution.py:603
  107.6 23.1 %collective-permute-start.17 = (f32[14,48,128]{2,1,0:T(8,128)S(1)}, f32[14,48,128]{2,1,0:T(8,128)S(1)}, u32[]{:S(2)}, u32[]{:S(2)}) collective-permute-start(f32[14,48,128]{2,1,0:T(8,128)S(1)} %get-tuple-element.81), channel_id=1, source_target_pairs={{0,24},{8,16},{16,8},{24,0},{1,25},{9,17},{17,9},{25,1},{2,26},{10... | collective-permute-start | bytes 1032200 | tf_op jit(solution)/shard_map/ppermute | solution.py:603
  109.0 29.0 %collective-permute-start.18 = (f32[14,48,128]{2,1,0:T(8,128)S(1)}, f32[14,48,128]{2,1,0:T(8,128)S(1)}, u32[]{:S(2)}, u32[]{:S(2)}) collective-permute-start(f32[14,48,128]{2,1,0:T(8,128)S(1)} %get-tuple-element.82), channel_id=1, source_target_pairs={{0,16},{8,24},{16,0},{24,8},{1,17},{9,25},{17,1},{25,9},{2,18},{10... | collective-permute-start | bytes 1032200 | tf_op jit(solution)/shard_map/ppermute | solution.py:603
  115.9 23.7 %collective-permute-start.19 = (f32[14,48,128]{2,1,0:T(8,128)S(1)}, f32[14,48,128]{2,1,0:T(8,128)S(1)}, u32[]{:S(2)}, u32[]{:S(2)}) collective-permute-start(f32[14,48,128]{2,1,0:T(8,128)S(1)} %get-tuple-element.83), channel_id=1, source_target_pairs={{0,8},{8,0},{16,24},{24,16},{1,9},{9,1},{17,25},{25,17},{2,10},{10... | collective-permute-start | bytes 1032200 | tf_op jit(solution)/shard_map/ppermute | solution.py:603
  123.3 22.1 %collective-permute-start.12 = (f32[14,48,128]{2,1,0:T(8,128)S(1)}, f32[14,48,128]{2,1,0:T(8,128)S(1)}, u32[]{:S(2)}, u32[]{:S(2)}) collective-permute-start(f32[14,48,128]{2,1,0:T(8,128)S(1)} %get-tuple-element.74), channel_id=1, source_target_pairs={{0,24},{8,16},{16,8},{24,0},{1,25},{9,17},{17,9},{25,1},{2,26},{10... | collective-permute-start | bytes 1032200 | tf_op jit(solution)/shard_map/ppermute | solution.py:603
  124.8 27.9 %collective-permute-start.13 = (f32[14,48,128]{2,1,0:T(8,128)S(1)}, f32[14,48,128]{2,1,0:T(8,128)S(1)}, u32[]{:S(2)}, u32[]{:S(2)}) collective-permute-start(f32[14,48,128]{2,1,0:T(8,128)S(1)} %get-tuple-element.75), channel_id=1, source_target_pairs={{0,16},{8,24},{16,0},{24,8},{1,17},{9,25},{17,1},{25,9},{2,18},{10... | collective-permute-start | bytes 1032200 | tf_op jit(solution)/shard_map/ppermute | solution.py:603
  130.7 23.6 %collective-permute-start.14 = (f32[14,48,128]{2,1,0:T(8,128)S(1)}, f32[14,48,128]{2,1,0:T(8,128)S(1)}, u32[]{:S(2)}, u32[]{:S(2)}) collective-permute-start(f32[14,48,128]{2,1,0:T(8,128)S(1)} %get-tuple-element.76), channel_id=1, source_target_pairs={{0,8},{8,0},{16,24},{24,16},{1,9},{9,1},{17,25},{25,17},{2,10},{10... | collective-permute-start | bytes 1032200 | tf_op jit(solution)/shard_map/ppermute | solution.py:603
  138.1 22.2 %collective-permute-start.7 = (f32[14,48,128]{2,1,0:T(8,128)S(1)}, f32[14,48,128]{2,1,0:T(8,128)S(1)}, u32[]{:S(2)}, u32[]{:S(2)}) collective-permute-start(f32[14,48,128]{2,1,0:T(8,128)S(1)} %get-tuple-element.67), channel_id=1, source_target_pairs={{0,24},{8,16},{16,8},{24,0},{1,25},{9,17},{17,9},{25,1},{2,26},{10... | collective-permute-start | bytes 1032200 | tf_op jit(solution)/shard_map/ppermute | solution.py:603
  139.6 27.5 %collective-permute-start.8 = (f32[14,48,128]{2,1,0:T(8,128)S(1)}, f32[14,48,128]{2,1,0:T(8,128)S(1)}, u32[]{:S(2)}, u32[]{:S(2)}) collective-permute-start(f32[14,48,128]{2,1,0:T(8,128)S(1)} %get-tuple-element.68), channel_id=1, source_target_pairs={{0,16},{8,24},{16,0},{24,8},{1,17},{9,25},{17,1},{25,9},{2,18},{10... | collective-permute-start | bytes 1032200 | tf_op jit(solution)/shard_map/ppermute | solution.py:603
  145.5 22.2 %collective-permute-start.9 = (f32[14,48,128]{2,1,0:T(8,128)S(1)}, f32[14,48,128]{2,1,0:T(8,128)S(1)}, u32[]{:S(2)}, u32[]{:S(2)}) collective-permute-start(f32[14,48,128]{2,1,0:T(8,128)S(1)} %get-tuple-element.69), channel_id=1, source_target_pairs={{0,8},{8,0},{16,24},{24,16},{1,9},{9,1},{17,25},{25,17},{2,10},{10... | collective-permute-start | bytes 1032200 | tf_op jit(solution)/shard_map/ppermute | solution.py:603
  145.6 14.8 %copy-start.21 = (f32[8,256]{1,0:T(8,128)S(1)}, f32[8,256]{1,0:T(8,128)}, u32[]{:S(2)}) copy-start(f32[8,256]{1,0:T(8,128)} %param.9) | copy-start | bytes 24580
  145.6 14.8 %copy-start.22 = (f32[8,256]{1,0:T(8,128)S(1)}, f32[8,256]{1,0:T(8,128)}, u32[]{:S(2)}) copy-start(f32[8,256]{1,0:T(8,128)} %param.8) | copy-start | bytes 24580
  152.8 19.4 %collective-permute-start.27 = (f32[14,32,128]{2,1,0:T(8,128)S(1)}, f32[14,32,128]{2,1,0:T(8,128)S(1)}, u32[]{:S(2)}, u32[]{:S(2)}) collective-permute-start(f32[14,32,128]{2,1,0:T(8,128)S(1)} %get-tuple-element.98), channel_id=1, source_target_pairs={{0,24},{8,16},{16,8},{24,0},{1,25},{9,17},{17,9},{25,1},{2,26},{10... | collective-permute-start | bytes 688136 | tf_op jit(solution)/shard_map/ppermute | solution.py:603
  154.3 20.0 %collective-permute-start.28 = (f32[14,32,128]{2,1,0:T(8,128)S(1)}, f32[14,32,128]{2,1,0:T(8,128)S(1)}, u32[]{:S(2)}, u32[]{:S(2)}) collective-permute-start(f32[14,32,128]{2,1,0:T(8,128)S(1)} %get-tuple-element.99), channel_id=1, source_target_pairs={{0,16},{8,24},{16,0},{24,8},{1,17},{9,25},{17,1},{25,9},{2,18},{10... | collective-permute-start | bytes 688136 | tf_op jit(solution)/shard_map/ppermute | solution.py:603
  160.3 14.3 %collective-permute-start.29 = (f32[14,32,128]{2,1,0:T(8,128)S(1)}, f32[14,32,128]{2,1,0:T(8,128)S(1)}, u32[]{:S(2)}, u32[]{:S(2)}) collective-permute-start(f32[14,32,128]{2,1,0:T(8,128)S(1)} %get-tuple-element.100), channel_id=1, source_target_pairs={{0,8},{8,0},{16,24},{24,16},{1,9},{9,1},{17,25},{25,17},{2,10},{10... | collective-permute-start | bytes 688136 | tf_op jit(solution)/shard_map/ppermute | solution.py:603
  176.5 0.7 copy-start.19
  177.2 20.6 %collective-permute-start.30 = (f32[1544,128]{1,0:T(8,128)S(1)}, f32[1544,128]{1,0:T(8,128)}, u32[]{:S(2)}, u32[]{:S(2)}) collective-permute-start(f32[1544,128]{1,0:T(8,128)S(1)} %get-tuple-element.107.refs_1_), channel_id=1, source_target_pairs={{0,8},{8,0},{16,24},{24,16},{1,9},{9,1},{17,25},{25,17},{2,10},{10... | collective-permute-start | bytes 2371592 | tf_op jit(solution)/shard_map/ppermute | solution.py:603
  178.0 20.9 %collective-permute-start.32 = (f32[1544,128]{1,0:T(8,128)}, f32[1544,128]{1,0:T(8,128)S(1)}, u32[]{:S(2)}, u32[]{:S(2)}) collective-permute-start(f32[1544,128]{1,0:T(8,128)} %get-tuple-element.108.refs_2_), channel_id=1, source_target_pairs={{0,16},{8,24},{16,0},{24,8},{1,17},{9,25},{17,1},{25,9},{2,18},{10... | collective-permute-start | bytes 2371592 | tf_op jit(solution)/shard_map/ppermute | solution.py:603
  179.0 40.2 %collective-permute-start.34 = (f32[1544,128]{1,0:T(8,128)}, f32[1544,128]{1,0:T(8,128)}, u32[]{:S(2)}, u32[]{:S(2)}) collective-permute-start(f32[1544,128]{1,0:T(8,128)} %get-tuple-element.108.refs_2_), channel_id=1, source_target_pairs={{0,8},{8,0},{16,24},{24,16},{1,9},{9,1},{17,25},{25,17},{2,10},{10... | collective-permute-start | bytes 2371592 | tf_op jit(solution)/shard_map/ppermute | solution.py:603
  180.3 38.9 %collective-permute-start.35 = (f32[1544,128]{1,0:T(8,128)S(1)}, f32[1544,128]{1,0:T(8,128)}, u32[]{:S(2)}, u32[]{:S(2)}) collective-permute-start(f32[1544,128]{1,0:T(8,128)S(1)} %get-tuple-element.107.refs_1_), channel_id=1, source_target_pairs={{0,16},{8,24},{16,0},{24,8},{1,17},{9,25},{17,1},{25,9},{2,18},{10... | collective-permute-start | bytes 2371592 | tf_op jit(solution)/shard_map/ppermute | solution.py:603
  197.8 33.7 %collective-permute-start.31 = (f32[1544,128]{1,0:T(8,128)}, f32[1544,128]{1,0:T(8,128)}, u32[]{:S(2)}, u32[]{:S(2)}) collective-permute-start(f32[1544,128]{1,0:T(8,128)} %collective-permute-done.30.refs_3_), channel_id=1, source_target_pairs={{0,16},{8,24},{16,0},{24,8},{1,17},{9,25},{17,1},{25,9},{2,18},{10... | collective-permute-start | bytes 2371592 | tf_op jit(solution)/shard_map/ppermute | solution.py:603
  198.9 32.6 %collective-permute-start.33 = (f32[1544,128]{1,0:T(8,128)S(1)}, f32[1544,128]{1,0:T(8,128)}, u32[]{:S(2)}, u32[]{:S(2)}) collective-permute-start(f32[1544,128]{1,0:T(8,128)S(1)} %collective-permute-done.32.refs_6_.refs_3_), channel_id=1, source_target_pairs={{0,8},{8,0},{16,24},{24,16},{1,9},{9,1},{17,25},{25,17},{2,10},{10... | collective-permute-start | bytes 2371592 | tf_op jit(solution)/shard_map/ppermute | solution.py:603
  215.8 1.0 copy-start.20
where the time goes:
time: 237 us; the launch traced here: 236 us
  waiting for transfers between devices  109 us (46%)
  Pallas kernels  59.6 us (25%)
  starting transfers between devices  38.9 us (16%)
  blocking collectives  15.4 us (6%)
  local copies, waits for them, and re-layouts  12.2 us (5%)
    ppermute x24, waiting for transfers between devices, swap(): return lax.ppermute(x, 'mem', [(i, i ^ p) for i in range(parts)])  73.3 us
    pallas_call x6, Pallas kernels, forecast_chunk(): pl.pallas_call(functools.partial(forecast_body, begin=begin, rows=rows, s...  34 us
    ppermute x6, waiting for transfers between devices, halo(): prev = lax.ppermute(bot, 'tile', up)  26.1 us
    ppermute x24, starting transfers between devices, swap(): return lax.ppermute(x, 'mem', [(i, i ^ p) for i in range(parts)])  23.5 us
    psum x1, blocking collectives, step(): sums = lax.psum(jnp.sum(sums, axis=1)[None, :], 'tile')  15.4 us
    ppermute x6, starting transfers between devices, halo(): return (prev, top, bot, lax.ppermute(top, 'tile', down))  14 us
    pallas_call x2, Pallas kernels, update(): pl.pallas_call(body, grid_spec=pltpu.PrefetchScalarGridSpec(num_scalar_pr...  12.8 us
    unnamed x50, local copies, waits for them, and re-layouts  12.1 us
  transfers between devices with their start and end apart: 36, of which 19 were waited for; matrix products, arithmetic and copies ran while one was open for 1% of the time, Pallas kernels for 21%

commit v1 on v0

--- a/solution.py
+++ b/solution.py
@@ -14,10 +14,10 @@
 FIELDS = 3
 LANES = 128
 CHUNKS = 4
+AHEAD = 3
 VMEM_MIB = 22
 SPREAD_VMEM_MIB = 58
 REST_VMEM_MIB = 22
-FIRST = 2
 SPARE = 8
 HIGHEST = lax.Precision.HIGHEST
 
@@ -586,6 +586,10 @@
     return [(unit * begin, unit * size) for begin, size in shares]
 
 
+def spread_groups(count):
+    return [(0, AHEAD - 1), (AHEAD - 1, AHEAD), (AHEAD, count)]
+
+
 def step(ensemble, obs_cells, region_tile, obs_values, obs_error):
     members, _, rows, width = ensemble.shape
     parts = lax.axis_size("mem")
@@ -613,8 +617,10 @@
     cells = cells + lax.broadcasted_iota(jnp.int32, (FIELDS * rows, width, obs), 1)
     onehot = (cells == obs_index[None, None, :]).astype(BF16)
 
-    pairs = spread(flat, plan[:FIRST], rows, width, SPREAD_VMEM_MIB)
-    pairs += spread(flat, plan[FIRST:], rows, width, REST_VMEM_MIB)
+    pairs = []
+    for group, (begin, end) in enumerate(spread_groups(len(plan))):
+        mib = REST_VMEM_MIB if group == 2 else SPREAD_VMEM_MIB
+        pairs += spread(flat, plan[begin:end], rows, width, mib)
 
     def halo(chunk):
         top, bot = pairs[chunk]

time: 237 us -> 236 us (level)
  Pallas kernels: 59.6 us -> 62.6 us
  waiting for transfers between devices: 109 us -> 106 us
    pallas_call x2 -> x3, Pallas kernels: 4.82 us -> 7.02 us  [spread(): pl.pallas_call(functools.partial(spread_body, chunks=chunks, rows=rows),...]
    unnamed x50 -> x42, local copies, waits for them, and re-layouts: 12.1 us -> 10 us
  transfers between devices with their start and end apart: 36 -> 36, of which waited for: 19 -> 19; matrix products, arithmetic and copies ran while one was open for 1% -> 1% of each run, Pallas kernels for 21% -> 23%
where the time goes in v1:
time: 236 us; the launch traced here: 235 us
  waiting for transfers between devices  106 us (45%)
  Pallas kernels  62.6 us (27%)
  starting transfers between devices  38.9 us (16%)
  blocking collectives  15.4 us (7%)
  local copies, waits for them, and re-layouts  10.1 us (4%)
    ppermute x24, waiting for transfers between devices, swap(): return lax.ppermute(x, 'mem', [(i, i ^ p) for i in range(parts)])  72.2 us
    pallas_call x6, Pallas kernels, forecast_chunk(): pl.pallas_call(functools.partial(forecast_body, begin=begin, rows=rows, s...  34.8 us
    ppermute x6, waiting for transfers between devices, halo(): prev = lax.ppermute(bot, 'tile', up)  25.3 us
    ppermute x24, starting transfers between devices, swap(): return lax.ppermute(x, 'mem', [(i, i ^ p) for i in range(parts)])  23.5 us
    psum x1, blocking collectives, step(): sums = lax.psum(jnp.sum(sums, axis=1)[None, :], 'tile')  15.4 us
    ppermute x6, starting transfers between devices, halo(): return (prev, top, bot, lax.ppermute(top, 'tile', down))  14 us
    pallas_call x2, Pallas kernels, update(): pl.pallas_call(body, grid_spec=pltpu.PrefetchScalarGridSpec(num_scalar_pr...  12.8 us
    unnamed x42, local copies, waits for them, and re-layouts  10 us
  transfers between devices with their start and end apart: 36, of which 19 were waited for; matrix products, arithmetic and copies ran while one was open for 1% of the time, Pallas kernels for 23%

profile of v1, /device:TPU:0, one launch (start us, length us, event | category | flops | bytes accessed | tf_op | source)
XLA Modules:
  0.0 235.0 jit_solution(9121442717209469938)
XLA Ops:
  0.0 2.8 %spread.3 = (f32[12,32,256]{2,1,0:T(8,128)}, f32[12,32,256]{2,1,0:T(8,128)}, f32[12,48,256]{2,1,0:T(8,128)}, f32[12,48,256]{2,1,0:T(8,128)}) custom-call(f32[6144,256]{1,0:T(8,128)} %bitcast.6), custom_call_target="tpu_custom_call" | custom-call | tf_op jit(solution)/shard_map/spread/pallas_call | solution.py:85
  2.8 0.5 collective-permute-start.5
  3.4 4.1 %collective-permute-start.6 = (f32[12,48,256]{2,1,0:T(8,128)}, f32[12,48,256]{2,1,0:T(8,128)}, u32[]{:S(2)}, u32[]{:S(2)}) collective-permute-start(f32[12,48,256]{2,1,0:T(8,128)} %get-tuple-element.64.top_ref), channel_id=1, source_target_pairs={{1,0},{2,1},{3,2},{4,3},{5,4},{6,5},{7,6},{0,7},{9,8},{10,9},{11,1... | collective-permute-start | bytes 1769480 | tf_op jit(solution)/shard_map/ppermute | solution.py:628
  7.5 2.4 %spread.4 = (f32[12,48,256]{2,1,0:T(8,128)}, f32[12,48,256]{2,1,0:T(8,128)}) custom-call(f32[6144,256]{1,0:T(8,128)} %bitcast.7), custom_call_target="tpu_custom_call" | custom-call | tf_op jit(solution)/shard_map/spread/pallas_call | solution.py:85
  10.3 3.3 %collective-permute-start.1 = (f32[12,32,256]{2,1,0:T(8,128)S(1)}, f32[12,32,256]{2,1,0:T(8,128)S(1)}, u32[]{:S(2)}, u32[]{:S(2)}) collective-permute-start(f32[12,32,256]{2,1,0:T(8,128)S(1)} %copy-done.8), channel_id=1, source_target_pairs={{1,0},{2,1},{3,2},{4,3},{5,4},{6,5},{7,6},{0,7},{9,8},{10,9},{11,1... | collective-permute-start | bytes 1179656 | tf_op jit(solution)/shard_map/ppermute | solution.py:628
  13.6 2.8 %copy-done = f32[256,3,8,256]{3,2,1,0:T(8,128)S(1)} copy-done((f32[256,3,8,256]{3,2,1,0:T(8,128)S(1)}, f32[256,3,8,256]{3,2,1,0:T(8,128)}, u32[]{:S(2)}) %copy-start) | copy-done | bytes 6291480
  16.4 1.8 spread.5
  18.2 18.0 %collective-permute-done.prev_ref = f32[12,32,256]{2,1,0:T(8,128)S(1)} collective-permute-done((f32[12,32,256]{2,1,0:T(8,128)S(1)}, f32[12,32,256]{2,1,0:T(8,128)S(1)}, u32[]{:S(2)}, u32[]{:S(2)}) %collective-permute-start) | collective-permute-done | bytes 393248 | tf_op jit(solution)/shard_map/ppermute | solution.py:627
  36.3 0.8 copy-done.11
  37.0 0.7 copy-done.13
  37.8 0.5 collective-permute-start.15
  38.3 3.0 %collective-permute-start.16 = (f32[12,48,256]{2,1,0:T(8,128)}, f32[12,48,256]{2,1,0:T(8,128)}, u32[]{:S(2)}, u32[]{:S(2)}) collective-permute-start(f32[12,48,256]{2,1,0:T(8,128)} %copy-done.6), channel_id=1, source_target_pairs={{1,0},{2,1},{3,2},{4,3},{5,4},{6,5},{7,6},{0,7},{9,8},{10,9},{11,1... | collective-permute-start | bytes 1769480 | tf_op jit(solution)/shard_map/ppermute | solution.py:628
  41.3 3.5 %collective-permute-start.21 = (f32[12,48,256]{2,1,0:T(8,128)S(1)}, f32[12,48,256]{2,1,0:T(8,128)}, u32[]{:S(2)}, u32[]{:S(2)}) collective-permute-start(f32[12,48,256]{2,1,0:T(8,128)S(1)} %get-tuple-element.85.top_ref), channel_id=1, source_target_pairs={{1,0},{2,1},{3,2},{4,3},{5,4},{6,5},{7,6},{0,7},{9,8},{10,9},{11,1... | collective-permute-start | bytes 1769480 | tf_op jit(solution)/shard_map/ppermute | solution.py:628
  45.0 4.9 %collective-permute-done.11.next_ref = f32[12,48,256]{2,1,0:T(8,128)} collective-permute-done((f32[12,48,256]{2,1,0:T(8,128)S(1)}, f32[12,48,256]{2,1,0:T(8,128)}, u32[]{:S(2)}, u32[]{:S(2)}) %collective-permute-start.11) | collective-permute-done | bytes 589856 | tf_op jit(solution)/shard_map/ppermute | solution.py:628
  49.9 5.6 %collective-permute-done.15.prev_ref = f32[12,48,256]{2,1,0:T(8,128)} collective-permute-done((f32[12,48,256]{2,1,0:T(8,128)}, f32[12,48,256]{2,1,0:T(8,128)}, u32[]{:S(2)}, u32[]{:S(2)}) %collective-permute-start.15) | collective-permute-done | bytes 589856 | tf_op jit(solution)/shard_map/ppermute | solution.py:627
  55.5 0.9 fusion.onehot_ref
  56.5 1.0 copy-done.10
  57.5 1.0 copy-done.12
  58.5 1.0 copy-done.14
  59.4 4.0 %forecast.6 = (f32[48,2048,128]{2,1,0:T(8,128)}, f32[14,32,128]{2,1,0:T(8,128)S(1)}, f32[14,32,128]{2,1,0:T(8,128)S(1)}, f32[14,32,128]{2,1,0:T(8,128)S(1)}, f32[14,32,128]{2,1,0:T(8,128)S(1)}) custom-call(s32[1]{0:T(128)} %bitcast.me_ref, f32[12,32,256]{2,1,0:T(8,128)S(1)} %copy-done.12, f32[12,32,256]{2,1,0:T(8,128)S(1)} %copy-done.8, ...), custom_call_target="tpu_custom_call" | custom-call | flops 50000000 | bytes 8000000 | tf_op jit(solution)/shard_map/forecast/pallas_call | solution.py:234
  63.5 3.0 %collective-permute-start.2 = (f32[14,32,128]{2,1,0:T(8,128)S(1)}, f32[14,32,128]{2,1,0:T(8,128)S(1)}, u32[]{:S(2)}, u32[]{:S(2)}) collective-permute-start(f32[14,32,128]{2,1,0:T(8,128)S(1)} %get-tuple-element.60), channel_id=1, source_target_pairs={{0,24},{8,16},{16,8},{24,0},{1,25},{9,17},{17,9},{25,1},{2,26},{10... | collective-permute-start | bytes 688136 | tf_op jit(solution)/shard_map/ppermute | solution.py:607
  66.5 1.7 collective-permute-done.20.prev_ref
  68.2 2.0 collective-permute-start.3
  70.2 3.7 %collective-permute-done.21.next_ref = f32[12,48,256]{2,1,0:T(8,128)} collective-permute-done((f32[12,48,256]{2,1,0:T(8,128)S(1)}, f32[12,48,256]{2,1,0:T(8,128)}, u32[]{:S(2)}, u32[]{:S(2)}) %collective-permute-start.21) | collective-permute-done | bytes 589856 | tf_op jit(solution)/shard_map/ppermute | solution.py:628
  73.9 2.0 collective-permute-start.4
  75.9 1.1 copy-done.2
  77.0 6.5 %forecast.7 = (f32[48,2048,128]{2,1,0:T(8,128)}, f32[14,48,128]{2,1,0:T(8,128)S(1)}, f32[14,48,128]{2,1,0:T(8,128)S(1)}, f32[14,48,128]{2,1,0:T(8,128)S(1)}, f32[14,48,128]{2,1,0:T(8,128)S(1)}) custom-call(s32[1]{0:T(128)} %bitcast.me_ref, f32[12,48,256]{2,1,0:T(8,128)} %collective-permute-done.5.prev_ref, ...), custom_call_target="tpu_custom_call", output_to_operand_aliasing={{0}: (6, {})} | custom-call | flops 50000000 | bytes 8000000 | tf_op jit(solution)/shard_map/forecast/pallas_call | solution.py:234
  83.5 6.5 %forecast.8 = (f32[48,2048,128]{2,1,0:T(8,128)}, f32[14,48,128]{2,1,0:T(8,128)S(1)}, f32[14,48,128]{2,1,0:T(8,128)S(1)}, f32[14,48,128]{2,1,0:T(8,128)S(1)}, f32[14,48,128]{2,1,0:T(8,128)S(1)}) custom-call(s32[1]{0:T(128)} %bitcast.me_ref, f32[12,48,256]{2,1,0:T(8,128)} %collective-permute-done.10.prev_ref, ...), custom_call_target="tpu_custom_call", output_to_operand_aliasing={{0}: (6, {})} | custom-call | flops 50000000 | bytes 8000000 | tf_op jit(solution)/shard_map/forecast/pallas_call | solution.py:234
  89.9 6.5 %forecast.9 = (f32[48,2048,128]{2,1,0:T(8,128)}, f32[14,48,128]{2,1,0:T(8,128)S(1)}, f32[14,48,128]{2,1,0:T(8,128)S(1)}, f32[14,48,128]{2,1,0:T(8,128)S(1)}, f32[14,48,128]{2,1,0:T(8,128)S(1)}) custom-call(s32[1]{0:T(128)} %bitcast.me_ref, f32[12,48,256]{2,1,0:T(8,128)} %collective-permute-done.15.prev_ref, ...), custom_call_target="tpu_custom_call", output_to_operand_aliasing={{0}: (6, {})} | custom-call | flops 50000000 | bytes 8000000 | tf_op jit(solution)/shard_map/forecast/pallas_call | solution.py:234
  96.4 6.4 %forecast.10 = (f32[48,2048,128]{2,1,0:T(8,128)}, f32[14,48,128]{2,1,0:T(8,128)S(1)}, f32[14,48,128]{2,1,0:T(8,128)S(1)}, f32[14,48,128]{2,1,0:T(8,128)S(1)}, f32[14,48,128]{2,1,0:T(8,128)S(1)}) custom-call(s32[1]{0:T(128)} %bitcast.me_ref, f32[12,48,256]{2,1,0:T(8,128)} %collective-permute-done.20.prev_ref, ...), custom_call_target="tpu_custom_call", output_to_operand_aliasing={{0}: (6, {})} | custom-call | flops 50000000 | bytes 8000000 | tf_op jit(solution)/shard_map/forecast/pallas_call | solution.py:234
  102.9 1.6 collective-permute-start.22
  104.5 1.9 collective-permute-start.24
  106.4 1.5 collective-permute-start.17
  108.0 6.7 %collective-permute-done.22.refs_17_ = f32[14,48,128]{2,1,0:T(8,128)S(1)} collective-permute-done((f32[14,48,128]{2,1,0:T(8,128)S(1)}, f32[14,48,128]{2,1,0:T(8,128)S(1)}, u32[]{:S(2)}, u32[]{:S(2)}) %collective-permute-start.22) | collective-permute-done | bytes 344096 | tf_op jit(solution)/shard_map/ppermute | solution.py:607
  114.9 7.3 %collective-permute-done.23.refs_18_ = f32[14,48,128]{2,1,0:T(8,128)S(1)} collective-permute-done((f32[14,48,128]{2,1,0:T(8,128)S(1)}, f32[14,48,128]{2,1,0:T(8,128)S(1)}, u32[]{:S(2)}, u32[]{:S(2)}) %collective-permute-start.23) | collective-permute-done | bytes 344096 | tf_op jit(solution)/shard_map/ppermute | solution.py:607
  122.2 1.5 collective-permute-start.12
  123.8 5.8 %collective-permute-done.17.refs_13_ = f32[14,48,128]{2,1,0:T(8,128)S(1)} collective-permute-done((f32[14,48,128]{2,1,0:T(8,128)S(1)}, f32[14,48,128]{2,1,0:T(8,128)S(1)}, u32[]{:S(2)}, u32[]{:S(2)}) %collective-permute-start.17) | collective-permute-done | bytes 344096 | tf_op jit(solution)/shard_map/ppermute | solution.py:607
  129.7 7.3 %collective-permute-done.18.refs_14_ = f32[14,48,128]{2,1,0:T(8,128)S(1)} collective-permute-done((f32[14,48,128]{2,1,0:T(8,128)S(1)}, f32[14,48,128]{2,1,0:T(8,128)S(1)}, u32[]{:S(2)}, u32[]{:S(2)}) %collective-permute-start.18) | collective-permute-done | bytes 344096 | tf_op jit(solution)/shard_map/ppermute | solution.py:607
  137.0 1.5 collective-permute-start.7
  138.5 5.8 %collective-permute-done.12.refs_9_ = f32[14,48,128]{2,1,0:T(8,128)S(1)} collective-permute-done((f32[14,48,128]{2,1,0:T(8,128)S(1)}, f32[14,48,128]{2,1,0:T(8,128)S(1)}, u32[]{:S(2)}, u32[]{:S(2)}) %collective-permute-start.12) | collective-permute-done | bytes 344096 | tf_op jit(solution)/shard_map/ppermute | solution.py:607
  144.5 5.0 %forecast.11 = (f32[48,2048,128]{2,1,0:T(8,128)}, f32[14,32,128]{2,1,0:T(8,128)S(1)}, f32[14,32,128]{2,1,0:T(8,128)S(1)}, f32[14,32,128]{2,1,0:T(8,128)S(1)}, f32[14,32,128]{2,1,0:T(8,128)S(1)}) custom-call(s32[1]{0:T(128)} %bitcast.me_ref, f32[12,32,256]{2,1,0:T(8,128)S(1)} %collective-permute-done.25.prev_ref, ...), custom_call_target="tpu_custom_call", output_to_operand_aliasing={{0}: (6, {})} | custom-call | flops 50000000 | bytes 8000000 | tf_op jit(solution)/shard_map/forecast/pallas_call | solution.py:234
  149.5 2.2 collective-permute-done.13.refs_10_
  151.7 1.5 collective-permute-start.27
  153.2 5.9 %collective-permute-done.7.refs_5_ = f32[14,48,128]{2,1,0:T(8,128)S(1)} collective-permute-done((f32[14,48,128]{2,1,0:T(8,128)S(1)}, f32[14,48,128]{2,1,0:T(8,128)S(1)}, u32[]{:S(2)}, u32[]{:S(2)}) %collective-permute-start.7) | collective-permute-done | bytes 344096 | tf_op jit(solution)/shard_map/ppermute | solution.py:607
  159.3 6.3 %collective-permute-done.8.refs_6_ = f32[14,48,128]{2,1,0:T(8,128)S(1)} collective-permute-done((f32[14,48,128]{2,1,0:T(8,128)S(1)}, f32[14,48,128]{2,1,0:T(8,128)S(1)}, u32[]{:S(2)}, u32[]{:S(2)}) %collective-permute-start.8) | collective-permute-done | bytes 344096 | tf_op jit(solution)/shard_map/ppermute | solution.py:607
  165.7 0.9 collective-permute-done.9.refs_7_
  166.6 3.6 %early.1 = (f32[14,256,128]{2,1,0:T(8,128)S(1)}, f32[14,128]{1,0:T(8,128)S(1)}, f32[2,256]{1,0:T(2,128)S(1)}) custom-call(f32[14,32,128]{2,1,0:T(8,128)S(1)} %get-tuple-element.59.refs_0_.refs_1_, f32[14,32,128]{2,1,0:T(8,128)S(1)} %collective-permute-done.2.refs_1_, f32[14,32,128]{2,1,0:T(8,128)S(1)} %collective-permute-done.3.refs_2_, ...), custom_call_target="tpu_custom_call" | custom-call | flops 10000000 | bytes 8000000 | tf_op jit(solution)/shard_map/early/pallas_call | solution.py:311
  170.1 0.6 collective-permute-done.27.refs_1_
  170.7 2.2 collective-permute-done.28.refs_2_
  173.2 2.0 late.1
  175.1 0.7 copy-done.15
  175.8 0.8 collective-permute-start.30
  176.7 1.0 collective-permute-start.32
  177.7 1.3 collective-permute-start.34
  179.0 0.9 collective-permute-start.35
  179.9 16.6 %collective-permute-done.30.refs_3_ = f32[1544,128]{1,0:T(8,128)} collective-permute-done((f32[1544,128]{1,0:T(8,128)S(1)}, f32[1544,128]{1,0:T(8,128)}, u32[]{:S(2)}, u32[]{:S(2)}) %collective-permute-start.30) | collective-permute-done | bytes 790560 | tf_op jit(solution)/shard_map/ppermute | solution.py:607
  196.4 1.1 collective-permute-start.31
  197.6 1.0 collective-permute-start.33
  199.0 15.4 %psum.7.sums_ref = f32[1,2]{1,0:T(1,128)S(1)} all-reduce(f32[1,2]{1,0:T(1,128)S(1)} %bitcast.15), channel_id=1, replica_groups=mesh['mem'=4,'tile'=8] {'tile'}, use_global_device_ids=true, to_apply=%region_4.5 | all-reduce | flops 2 | bytes 16 | tf_op jit(solution)/shard_map/psum | solution.py:648
  214.4 0.9 copy-done.16
  215.4 2.5 %weights.1 = (f32[256,256]{1,0:T(8,128)S(1)}, f32[8,128]{1,0:T(8,128)S(1)}) custom-call(f32[1,2]{1,0:T(1,128)S(1)} %psum.7.sums_ref, f32[1,256]{1,0:T(1,128)S(1)} %bitcast.12, f32[1,256]{1,0:T(1,128)S(1)} %bitcast.10, f32[8,256]{1,0:T(8,128)S(1)} %get-tuple-element.102.mean_ref, f32[256,256]{1,0:T(8,128)S(1)} %copy-done.16, ...), custom_call_target="tpu_custom_call" | custom-call | flops 10000000 | bytes 2000000 | tf_op jit(solution)/shard_map/weights/pallas_call | solution.py:462
  217.9 7.9 %update.1.refs_4_ = f32[256,3,8,256]{3,2,1,0:T(8,128)} custom-call(s32[4]{0:T(128)S(1)} %pad_add_fusion.2.tiles_ref, s32[6]{0:T(128)S(1)} %concatenate.15.owner_ref, f32[8,128]{1,0:T(8,128)S(1)} %get-tuple-element.104.scale_ref, f32[256,256]{1,0:T(8,128)S(1)} %get-tuple-element.105.weights_ref, f32[6,8,2048,128]{3,2,1,0:T(8,128)} %bitcast.13, ...), custom_call_target="tpu_custom_call" | custom-call | flops 10000000 | bytes 20000000 | tf_op jit(solution)/shard_map/update/pallas_call | solution.py:545
  225.8 4.3 %collective-permute-done.31.refs_1_ = f32[1544,128]{1,0:T(8,128)} collective-permute-done((f32[1544,128]{1,0:T(8,128)}, f32[1544,128]{1,0:T(8,128)}, u32[]{:S(2)}, u32[]{:S(2)}) %collective-permute-start.31) | collective-permute-done | bytes 790560 | tf_op jit(solution)/shard_map/ppermute | solution.py:607
  230.1 4.9 %finish.1 = f32[256,3,8,256]{3,2,1,0:T(8,128)} custom-call(s32[2]{0:T(128)S(1)} %pad_add_fusion.tiles_ref, s32[3]{0:T(128)S(1)} %pad_add_fusion.1.owner_ref, f32[8,128]{1,0:T(8,128)S(1)} %get-tuple-element.104.scale_ref, f32[256,256]{1,0:T(8,128)S(1)} %get-tuple-element.105.weights_ref, ...), custom_call_target="tpu_custom_call", output_to_operand_aliasing={{}: (8, {})} | custom-call | flops 10000000 | bytes 20000000 | tf_op jit(solution)/shard_map/finish/pallas_call | solution.py:545
  (75 shorter events, 2.2 us)
Async XLA Ops:
  2.8 7.2 %copy-start.9 = (f32[12,32,256]{2,1,0:T(8,128)S(1)}, f32[12,32,256]{2,1,0:T(8,128)}, u32[]{:S(2)}) copy-start(f32[12,32,256]{2,1,0:T(8,128)} %get-tuple-element.57.bot_ref) | copy-start | bytes 1179652
  2.8 7.5 %copy-start.8 = (f32[12,32,256]{2,1,0:T(8,128)S(1)}, f32[12,32,256]{2,1,0:T(8,128)}, u32[]{:S(2)}) copy-start(f32[12,32,256]{2,1,0:T(8,128)} %get-tuple-element.58.top_ref) | copy-start | bytes 1179652
  2.8 35.5 %collective-permute-start.5 = (f32[12,48,256]{2,1,0:T(8,128)}, f32[12,48,256]{2,1,0:T(8,128)}, u32[]{:S(2)}, u32[]{:S(2)}) collective-permute-start(f32[12,48,256]{2,1,0:T(8,128)} %get-tuple-element.63.bot_ref), channel_id=1, source_target_pairs={{0,1},{1,2},{2,3},{3,4},{4,5},{5,6},{6,7},{7,0},{8,9},{9,10},{10,1... | collective-permute-start | bytes 1769480 | tf_op jit(solution)/shard_map/ppermute | solution.py:627
  3.4 41.5 %copy-start.20 = (s32[8]{0:T(128)S(1)}, s32[8]{0:T(128)}, u32[]{:S(2)}) copy-start(s32[8]{0:T(128)} %param.7) | copy-start | bytes 100
  3.4 41.5 %copy-start.19 = (s32[8,256]{1,0:T(8,128)S(1)}, s32[8,256]{1,0:T(8,128)}, u32[]{:S(2)}) copy-start(s32[8,256]{1,0:T(8,128)} %param.6) | copy-start | bytes 24580
  3.4 38.0 %collective-permute-start.6 = (f32[12,48,256]{2,1,0:T(8,128)}, f32[12,48,256]{2,1,0:T(8,128)}, u32[]{:S(2)}, u32[]{:S(2)}) collective-permute-start(f32[12,48,256]{2,1,0:T(8,128)} %get-tuple-element.64.top_ref), channel_id=1, source_target_pairs={{1,0},{2,1},{3,2},{4,3},{5,4},{6,5},{7,6},{0,7},{9,8},{10,9},{11,1... | collective-permute-start | bytes 1769480 | tf_op jit(solution)/shard_map/ppermute | solution.py:628
  9.9 31.4 %collective-permute-start.10 = (f32[12,48,256]{2,1,0:T(8,128)}, f32[12,48,256]{2,1,0:T(8,128)}, u32[]{:S(2)}, u32[]{:S(2)}) collective-permute-start(f32[12,48,256]{2,1,0:T(8,128)} %get-tuple-element.70.bot_ref), channel_id=1, source_target_pairs={{0,1},{1,2},{2,3},{3,4},{4,5},{5,6},{6,7},{7,0},{8,9},{9,10},{10,1... | collective-permute-start | bytes 1769480 | tf_op jit(solution)/shard_map/ppermute | solution.py:627
  10.0 26.2 %collective-permute-start = (f32[12,32,256]{2,1,0:T(8,128)S(1)}, f32[12,32,256]{2,1,0:T(8,128)S(1)}, u32[]{:S(2)}, u32[]{:S(2)}) collective-permute-start(f32[12,32,256]{2,1,0:T(8,128)S(1)} %copy-done.9), channel_id=1, source_target_pairs={{0,1},{1,2},{2,3},{3,4},{4,5},{5,6},{6,7},{7,0},{8,9},{9,10},{10,1... | collective-permute-start | bytes 1179656 | tf_op jit(solution)/shard_map/ppermute | solution.py:627
  10.3 26.7 %collective-permute-start.1 = (f32[12,32,256]{2,1,0:T(8,128)S(1)}, f32[12,32,256]{2,1,0:T(8,128)S(1)}, u32[]{:S(2)}, u32[]{:S(2)}) collective-permute-start(f32[12,32,256]{2,1,0:T(8,128)S(1)} %copy-done.8), channel_id=1, source_target_pairs={{1,0},{2,1},{3,2},{4,3},{5,4},{6,5},{7,6},{0,7},{9,8},{10,9},{11,1... | collective-permute-start | bytes 1179656 | tf_op jit(solution)/shard_map/ppermute | solution.py:628
  13.6 2.8 %copy-start = (f32[256,3,8,256]{3,2,1,0:T(8,128)S(1)}, f32[256,3,8,256]{3,2,1,0:T(8,128)}, u32[]{:S(2)}) copy-start(f32[256,3,8,256]{3,2,1,0:T(8,128)} %param.5) | copy-start | bytes 18874372
  16.4 20.6 %copy-start.3 = (f32[12,48,256]{2,1,0:T(8,128)S(1)}, f32[12,48,256]{2,1,0:T(8,128)}, u32[]{:S(2)}) copy-start(f32[12,48,256]{2,1,0:T(8,128)} %get-tuple-element.71.top_ref) | copy-start | bytes 1769476
  16.4 59.5 %copy-start.1 = (f32[12,48,256]{2,1,0:T(8,128)S(1)}, f32[12,48,256]{2,1,0:T(8,128)}, u32[]{:S(2)}) copy-start(f32[12,48,256]{2,1,0:T(8,128)} %get-tuple-element.64.top_ref) | copy-start | bytes 1769476
  18.2 18.8 %copy-start.6 = (f32[12,48,256]{2,1,0:T(8,128)}, f32[12,48,256]{2,1,0:T(8,128)S(1)}, u32[]{:S(2)}) copy-start(f32[12,48,256]{2,1,0:T(8,128)S(1)} %get-tuple-element.78.top_ref) | copy-start | bytes 1769476
  36.2 0.8 copy-start.11
  37.0 12.9 %collective-permute-start.11 = (f32[12,48,256]{2,1,0:T(8,128)S(1)}, f32[12,48,256]{2,1,0:T(8,128)}, u32[]{:S(2)}, u32[]{:S(2)}) collective-permute-start(f32[12,48,256]{2,1,0:T(8,128)S(1)} %copy-done.3), channel_id=1, source_target_pairs={{1,0},{2,1},{3,2},{4,3},{5,4},{6,5},{7,6},{0,7},{9,8},{10,9},{11,1... | collective-permute-start | bytes 1769480 | tf_op jit(solution)/shard_map/ppermute | solution.py:628
  37.0 0.8 copy-start.13
  37.8 17.7 %collective-permute-start.15 = (f32[12,48,256]{2,1,0:T(8,128)}, f32[12,48,256]{2,1,0:T(8,128)}, u32[]{:S(2)}, u32[]{:S(2)}) collective-permute-start(f32[12,48,256]{2,1,0:T(8,128)} %get-tuple-element.77.bot_ref), channel_id=1, source_target_pairs={{0,1},{1,2},{2,3},{3,4},{4,5},{5,6},{6,7},{7,0},{8,9},{9,10},{10,1... | collective-permute-start | bytes 1769480 | tf_op jit(solution)/shard_map/ppermute | solution.py:627
  38.3 25.2 %collective-permute-start.16 = (f32[12,48,256]{2,1,0:T(8,128)}, f32[12,48,256]{2,1,0:T(8,128)}, u32[]{:S(2)}, u32[]{:S(2)}) collective-permute-start(f32[12,48,256]{2,1,0:T(8,128)} %copy-done.6), channel_id=1, source_target_pairs={{1,0},{2,1},{3,2},{4,3},{5,4},{6,5},{7,6},{0,7},{9,8},{10,9},{11,1... | collective-permute-start | bytes 1769480 | tf_op jit(solution)/shard_map/ppermute | solution.py:628
  41.3 26.8 %collective-permute-start.20 = (f32[12,48,256]{2,1,0:T(8,128)S(1)}, f32[12,48,256]{2,1,0:T(8,128)}, u32[]{:S(2)}, u32[]{:S(2)}) collective-permute-start(f32[12,48,256]{2,1,0:T(8,128)S(1)} %get-tuple-element.84.bot_ref), channel_id=1, source_target_pairs={{0,1},{1,2},{2,3},{3,4},{4,5},{5,6},{6,7},{7,0},{8,9},{9,10},{10,1... | collective-permute-start | bytes 1769480 | tf_op jit(solution)/shard_map/ppermute | solution.py:627
  41.3 32.6 %collective-permute-start.21 = (f32[12,48,256]{2,1,0:T(8,128)S(1)}, f32[12,48,256]{2,1,0:T(8,128)}, u32[]{:S(2)}, u32[]{:S(2)}) collective-permute-start(f32[12,48,256]{2,1,0:T(8,128)S(1)} %get-tuple-element.85.top_ref), channel_id=1, source_target_pairs={{1,0},{2,1},{3,2},{4,3},{5,4},{6,5},{7,6},{0,7},{9,8},{10,9},{11,1... | collective-permute-start | bytes 1769480 | tf_op jit(solution)/shard_map/ppermute | solution.py:628
  49.9 52.9 %collective-permute-start.25 = (f32[12,32,256]{2,1,0:T(8,128)}, f32[12,32,256]{2,1,0:T(8,128)S(1)}, u32[]{:S(2)}, u32[]{:S(2)}) collective-permute-start(f32[12,32,256]{2,1,0:T(8,128)} %get-tuple-element.94.bot_ref), channel_id=1, source_target_pairs={{0,1},{1,2},{2,3},{3,4},{4,5},{5,6},{6,7},{7,0},{8,9},{9,10},{10,1... | collective-permute-start | bytes 1179656 | tf_op jit(solution)/shard_map/ppermute | solution.py:627
  55.5 48.9 %collective-permute-start.26 = (f32[12,32,256]{2,1,0:T(8,128)S(1)}, f32[12,32,256]{2,1,0:T(8,128)S(1)}, u32[]{:S(2)}, u32[]{:S(2)}) collective-permute-start(f32[12,32,256]{2,1,0:T(8,128)S(1)} %get-tuple-element.95.top_ref), channel_id=1, source_target_pairs={{1,0},{2,1},{3,2},{4,3},{5,4},{6,5},{7,6},{0,7},{9,8},{10,9},{11,1... | collective-permute-start | bytes 1179656 | tf_op jit(solution)/shard_map/ppermute | solution.py:628
  56.5 1.0 copy-start.10
  57.5 1.0 copy-start.12
  58.4 1.0 copy-start.14
  63.5 41.1 %collective-permute-start.2 = (f32[14,32,128]{2,1,0:T(8,128)S(1)}, f32[14,32,128]{2,1,0:T(8,128)S(1)}, u32[]{:S(2)}, u32[]{:S(2)}) collective-permute-start(f32[14,32,128]{2,1,0:T(8,128)S(1)} %get-tuple-element.60), channel_id=1, source_target_pairs={{0,24},{8,16},{16,8},{24,0},{1,25},{9,17},{17,9},{25,1},{2,26},{10... | collective-permute-start | bytes 688136 | tf_op jit(solution)/shard_map/ppermute | solution.py:607
  68.2 38.3 %collective-permute-start.3 = (f32[14,32,128]{2,1,0:T(8,128)S(1)}, f32[14,32,128]{2,1,0:T(8,128)S(1)}, u32[]{:S(2)}, u32[]{:S(2)}) collective-permute-start(f32[14,32,128]{2,1,0:T(8,128)S(1)} %get-tuple-element.61), channel_id=1, source_target_pairs={{0,16},{8,24},{16,0},{24,8},{1,17},{9,25},{17,1},{25,9},{2,18},{10... | collective-permute-start | bytes 688136 | tf_op jit(solution)/shard_map/ppermute | solution.py:607
  73.9 34.0 %collective-permute-start.4 = (f32[14,32,128]{2,1,0:T(8,128)S(1)}, f32[14,32,128]{2,1,0:T(8,128)S(1)}, u32[]{:S(2)}, u32[]{:S(2)}) collective-permute-start(f32[14,32,128]{2,1,0:T(8,128)S(1)} %get-tuple-element.62), channel_id=1, source_target_pairs={{0,8},{8,0},{16,24},{24,16},{1,9},{9,1},{17,25},{25,17},{2,10},{10... | collective-permute-start | bytes 688136 | tf_op jit(solution)/shard_map/ppermute | solution.py:607
  75.9 1.1 copy-start.2
  77.0 6.5 %copy-start.4 = (f32[12,48,256]{2,1,0:T(8,128)S(1)}, f32[12,48,256]{2,1,0:T(8,128)}, u32[]{:S(2)}) copy-start(f32[12,48,256]{2,1,0:T(8,128)} %get-tuple-element.71.top_ref) | copy-start | bytes 1769476
  77.0 6.5 %copy-start.5 = (f32[12,48,256]{2,1,0:T(8,128)S(1)}, f32[12,48,256]{2,1,0:T(8,128)}, u32[]{:S(2)}) copy-start(f32[12,48,256]{2,1,0:T(8,128)} %get-tuple-element.70.bot_ref) | copy-start | bytes 1769476
  83.5 6.5 %copy-start.7 = (f32[12,48,256]{2,1,0:T(8,128)S(1)}, f32[12,48,256]{2,1,0:T(8,128)}, u32[]{:S(2)}) copy-start(f32[12,48,256]{2,1,0:T(8,128)} %copy-done.6) | copy-start | bytes 1769476
  102.9 11.9 %collective-permute-start.22 = (f32[14,48,128]{2,1,0:T(8,128)S(1)}, f32[14,48,128]{2,1,0:T(8,128)S(1)}, u32[]{:S(2)}, u32[]{:S(2)}) collective-permute-start(f32[14,48,128]{2,1,0:T(8,128)S(1)} %get-tuple-element.88), channel_id=1, source_target_pairs={{0,24},{8,16},{16,8},{24,0},{1,25},{9,17},{17,9},{25,1},{2,26},{10... | collective-permute-start | bytes 1032200 | tf_op jit(solution)/shard_map/ppermute | solution.py:607
  104.4 17.8 %collective-permute-start.23 = (f32[14,48,128]{2,1,0:T(8,128)S(1)}, f32[14,48,128]{2,1,0:T(8,128)S(1)}, u32[]{:S(2)}, u32[]{:S(2)}) collective-permute-start(f32[14,48,128]{2,1,0:T(8,128)S(1)} %get-tuple-element.89), channel_id=1, source_target_pairs={{0,16},{8,24},{16,0},{24,8},{1,17},{9,25},{17,1},{25,9},{2,18},{10... | collective-permute-start | bytes 1032200 | tf_op jit(solution)/shard_map/ppermute | solution.py:607
  104.5 19.1 %collective-permute-start.24 = (f32[14,48,128]{2,1,0:T(8,128)S(1)}, f32[14,48,128]{2,1,0:T(8,128)S(1)}, u32[]{:S(2)}, u32[]{:S(2)}) collective-permute-start(f32[14,48,128]{2,1,0:T(8,128)S(1)} %get-tuple-element.90), channel_id=1, source_target_pairs={{0,8},{8,0},{16,24},{24,16},{1,9},{9,1},{17,25},{25,17},{2,10},{10... | collective-permute-start | bytes 1032200 | tf_op jit(solution)/shard_map/ppermute | solution.py:607
  106.4 23.1 %collective-permute-start.17 = (f32[14,48,128]{2,1,0:T(8,128)S(1)}, f32[14,48,128]{2,1,0:T(8,128)S(1)}, u32[]{:S(2)}, u32[]{:S(2)}) collective-permute-start(f32[14,48,128]{2,1,0:T(8,128)S(1)} %get-tuple-element.81), channel_id=1, source_target_pairs={{0,24},{8,16},{16,8},{24,0},{1,25},{9,17},{17,9},{25,1},{2,26},{10... | collective-permute-start | bytes 1032200 | tf_op jit(solution)/shard_map/ppermute | solution.py:607
  107.9 29.0 %collective-permute-start.18 = (f32[14,48,128]{2,1,0:T(8,128)S(1)}, f32[14,48,128]{2,1,0:T(8,128)S(1)}, u32[]{:S(2)}, u32[]{:S(2)}) collective-permute-start(f32[14,48,128]{2,1,0:T(8,128)S(1)} %get-tuple-element.82), channel_id=1, source_target_pairs={{0,16},{8,24},{16,0},{24,8},{1,17},{9,25},{17,1},{25,9},{2,18},{10... | collective-permute-start | bytes 1032200 | tf_op jit(solution)/shard_map/ppermute | solution.py:607
  114.8 23.7 %collective-permute-start.19 = (f32[14,48,128]{2,1,0:T(8,128)S(1)}, f32[14,48,128]{2,1,0:T(8,128)S(1)}, u32[]{:S(2)}, u32[]{:S(2)}) collective-permute-start(f32[14,48,128]{2,1,0:T(8,128)S(1)} %get-tuple-element.83), channel_id=1, source_target_pairs={{0,8},{8,0},{16,24},{24,16},{1,9},{9,1},{17,25},{25,17},{2,10},{10... | collective-permute-start | bytes 1032200 | tf_op jit(solution)/shard_map/ppermute | solution.py:607
  122.2 22.1 %collective-permute-start.12 = (f32[14,48,128]{2,1,0:T(8,128)S(1)}, f32[14,48,128]{2,1,0:T(8,128)S(1)}, u32[]{:S(2)}, u32[]{:S(2)}) collective-permute-start(f32[14,48,128]{2,1,0:T(8,128)S(1)} %get-tuple-element.74), channel_id=1, source_target_pairs={{0,24},{8,16},{16,8},{24,0},{1,25},{9,17},{17,9},{25,1},{2,26},{10... | collective-permute-start | bytes 1032200 | tf_op jit(solution)/shard_map/ppermute | solution.py:607
  123.7 28.0 %collective-permute-start.13 = (f32[14,48,128]{2,1,0:T(8,128)S(1)}, f32[14,48,128]{2,1,0:T(8,128)S(1)}, u32[]{:S(2)}, u32[]{:S(2)}) collective-permute-start(f32[14,48,128]{2,1,0:T(8,128)S(1)} %get-tuple-element.75), channel_id=1, source_target_pairs={{0,16},{8,24},{16,0},{24,8},{1,17},{9,25},{17,1},{25,9},{2,18},{10... | collective-permute-start | bytes 1032200 | tf_op jit(solution)/shard_map/ppermute | solution.py:607
  129.5 23.6 %collective-permute-start.14 = (f32[14,48,128]{2,1,0:T(8,128)S(1)}, f32[14,48,128]{2,1,0:T(8,128)S(1)}, u32[]{:S(2)}, u32[]{:S(2)}) collective-permute-start(f32[14,48,128]{2,1,0:T(8,128)S(1)} %get-tuple-element.76), channel_id=1, source_target_pairs={{0,8},{8,0},{16,24},{24,16},{1,9},{9,1},{17,25},{25,17},{2,10},{10... | collective-permute-start | bytes 1032200 | tf_op jit(solution)/shard_map/ppermute | solution.py:607
  137.0 22.1 %collective-permute-start.7 = (f32[14,48,128]{2,1,0:T(8,128)S(1)}, f32[14,48,128]{2,1,0:T(8,128)S(1)}, u32[]{:S(2)}, u32[]{:S(2)}) collective-permute-start(f32[14,48,128]{2,1,0:T(8,128)S(1)} %get-tuple-element.67), channel_id=1, source_target_pairs={{0,24},{8,16},{16,8},{24,0},{1,25},{9,17},{17,9},{25,1},{2,26},{10... | collective-permute-start | bytes 1032200 | tf_op jit(solution)/shard_map/ppermute | solution.py:607
  138.4 27.2 %collective-permute-start.8 = (f32[14,48,128]{2,1,0:T(8,128)S(1)}, f32[14,48,128]{2,1,0:T(8,128)S(1)}, u32[]{:S(2)}, u32[]{:S(2)}) collective-permute-start(f32[14,48,128]{2,1,0:T(8,128)S(1)} %get-tuple-element.68), channel_id=1, source_target_pairs={{0,16},{8,24},{16,0},{24,8},{1,17},{9,25},{17,1},{25,9},{2,18},{10... | collective-permute-start | bytes 1032200 | tf_op jit(solution)/shard_map/ppermute | solution.py:607
  144.3 22.2 %collective-permute-start.9 = (f32[14,48,128]{2,1,0:T(8,128)S(1)}, f32[14,48,128]{2,1,0:T(8,128)S(1)}, u32[]{:S(2)}, u32[]{:S(2)}) collective-permute-start(f32[14,48,128]{2,1,0:T(8,128)S(1)} %get-tuple-element.69), channel_id=1, source_target_pairs={{0,8},{8,0},{16,24},{24,16},{1,9},{9,1},{17,25},{25,17},{2,10},{10... | collective-permute-start | bytes 1032200 | tf_op jit(solution)/shard_map/ppermute | solution.py:607
  144.5 14.8 %copy-start.17 = (f32[8,256]{1,0:T(8,128)S(1)}, f32[8,256]{1,0:T(8,128)}, u32[]{:S(2)}) copy-start(f32[8,256]{1,0:T(8,128)} %param.9) | copy-start | bytes 24580
  144.5 14.8 %copy-start.18 = (f32[8,256]{1,0:T(8,128)S(1)}, f32[8,256]{1,0:T(8,128)}, u32[]{:S(2)}) copy-start(f32[8,256]{1,0:T(8,128)} %param.8) | copy-start | bytes 24580
  151.7 19.0 %collective-permute-start.27 = (f32[14,32,128]{2,1,0:T(8,128)S(1)}, f32[14,32,128]{2,1,0:T(8,128)S(1)}, u32[]{:S(2)}, u32[]{:S(2)}) collective-permute-start(f32[14,32,128]{2,1,0:T(8,128)S(1)} %get-tuple-element.98), channel_id=1, source_target_pairs={{0,24},{8,16},{16,8},{24,0},{1,25},{9,17},{17,9},{25,1},{2,26},{10... | collective-permute-start | bytes 688136 | tf_op jit(solution)/shard_map/ppermute | solution.py:607
  153.2 19.8 %collective-permute-start.28 = (f32[14,32,128]{2,1,0:T(8,128)S(1)}, f32[14,32,128]{2,1,0:T(8,128)S(1)}, u32[]{:S(2)}, u32[]{:S(2)}) collective-permute-start(f32[14,32,128]{2,1,0:T(8,128)S(1)} %get-tuple-element.99), channel_id=1, source_target_pairs={{0,16},{8,24},{16,0},{24,8},{1,17},{9,25},{17,1},{25,9},{2,18},{10... | collective-permute-start | bytes 688136 | tf_op jit(solution)/shard_map/ppermute | solution.py:607
  159.1 14.1 %collective-permute-start.29 = (f32[14,32,128]{2,1,0:T(8,128)S(1)}, f32[14,32,128]{2,1,0:T(8,128)S(1)}, u32[]{:S(2)}, u32[]{:S(2)}) collective-permute-start(f32[14,32,128]{2,1,0:T(8,128)S(1)} %get-tuple-element.100), channel_id=1, source_target_pairs={{0,8},{8,0},{16,24},{24,16},{1,9},{9,1},{17,25},{25,17},{2,10},{10... | collective-permute-start | bytes 688136 | tf_op jit(solution)/shard_map/ppermute | solution.py:607
  175.1 0.7 copy-start.15
  175.8 20.6 %collective-permute-start.30 = (f32[1544,128]{1,0:T(8,128)S(1)}, f32[1544,128]{1,0:T(8,128)}, u32[]{:S(2)}, u32[]{:S(2)}) collective-permute-start(f32[1544,128]{1,0:T(8,128)S(1)} %get-tuple-element.107.refs_1_), channel_id=1, source_target_pairs={{0,8},{8,0},{16,24},{24,16},{1,9},{9,1},{17,25},{25,17},{2,10},{10... | collective-permute-start | bytes 2371592 | tf_op jit(solution)/shard_map/ppermute | solution.py:607
  176.7 20.9 %collective-permute-start.32 = (f32[1544,128]{1,0:T(8,128)}, f32[1544,128]{1,0:T(8,128)S(1)}, u32[]{:S(2)}, u32[]{:S(2)}) collective-permute-start(f32[1544,128]{1,0:T(8,128)} %get-tuple-element.108.refs_2_), channel_id=1, source_target_pairs={{0,16},{8,24},{16,0},{24,8},{1,17},{9,25},{17,1},{25,9},{2,18},{10... | collective-permute-start | bytes 2371592 | tf_op jit(solution)/shard_map/ppermute | solution.py:607
  177.7 40.2 %collective-permute-start.34 = (f32[1544,128]{1,0:T(8,128)}, f32[1544,128]{1,0:T(8,128)}, u32[]{:S(2)}, u32[]{:S(2)}) collective-permute-start(f32[1544,128]{1,0:T(8,128)} %get-tuple-element.108.refs_2_), channel_id=1, source_target_pairs={{0,8},{8,0},{16,24},{24,16},{1,9},{9,1},{17,25},{25,17},{2,10},{10... | collective-permute-start | bytes 2371592 | tf_op jit(solution)/shard_map/ppermute | solution.py:607
  179.0 38.9 %collective-permute-start.35 = (f32[1544,128]{1,0:T(8,128)S(1)}, f32[1544,128]{1,0:T(8,128)}, u32[]{:S(2)}, u32[]{:S(2)}) collective-permute-start(f32[1544,128]{1,0:T(8,128)S(1)} %get-tuple-element.107.refs_1_), channel_id=1, source_target_pairs={{0,16},{8,24},{16,0},{24,8},{1,17},{9,25},{17,1},{25,9},{2,18},{10... | collective-permute-start | bytes 2371592 | tf_op jit(solution)/shard_map/ppermute | solution.py:607
  196.4 33.7 %collective-permute-start.31 = (f32[1544,128]{1,0:T(8,128)}, f32[1544,128]{1,0:T(8,128)}, u32[]{:S(2)}, u32[]{:S(2)}) collective-permute-start(f32[1544,128]{1,0:T(8,128)} %collective-permute-done.30.refs_3_), channel_id=1, source_target_pairs={{0,16},{8,24},{16,0},{24,8},{1,17},{9,25},{17,1},{25,9},{2,18},{10... | collective-permute-start | bytes 2371592 | tf_op jit(solution)/shard_map/ppermute | solution.py:607
  197.6 32.6 %collective-permute-start.33 = (f32[1544,128]{1,0:T(8,128)S(1)}, f32[1544,128]{1,0:T(8,128)}, u32[]{:S(2)}, u32[]{:S(2)}) collective-permute-start(f32[1544,128]{1,0:T(8,128)S(1)} %collective-permute-done.32.refs_6_.refs_3_), channel_id=1, source_target_pairs={{0,8},{8,0},{16,24},{24,16},{1,9},{9,1},{17,25},{25,17},{2,10},{10... | collective-permute-start | bytes 2371592 | tf_op jit(solution)/shard_map/ppermute | solution.py:607
  214.4 1.0 copy-start.16
